TPU v7x, 128 devices: a whole 4x4x4 slice. The times are simulated.
128 devices in a mesh: row: 8 (over y, x_hi), col: 16 (over z, x_lo, core).
Axes of the slice: x: 4 (x_hi: 2, x_lo: 2; x = x_hi * 2 + x_lo), y: 4, z: 4, core: 2. Of those that a mesh axis runs over, the one named last changes fastest.
Arguments:
- noise_points: float32 [32768, 512], P('row'), may hold values from -30 to 30
- data_points: float32 [4096, 512], P('col'), may hold values from -30 to 30
- times: float32 [32768, 8], P(('row', 'col')), may hold values from 0 to 1
- time_shift: float32 [1024], replicated, may hold values from -6 to 6
- weight_in: bfloat16 [512, 1024], replicated, may hold values from -0.25 to 0.25
- weight_out: bfloat16 [1024, 512], replicated, may hold values from -0.1875 to 0.1875
Outputs:
- predicted: bfloat16 [262144, 512], P(('row', 'col'))
- grad_in: float32 [512, 1024], replicated
- grad_out: float32 [1024, 512], replicated
All inputs are finite; a program needn't handle non-finite values.
Results may differ from a plain program's by a relative error of at most 0.0057.
Values sent between devices are 32-bit elements; how exact they have to be, the bound alone decides.
A program may use at most 128 MiB of HBM per device.

v0:
```python
import math

import jax
import jax.numpy as jnp
from jax import lax
from jax.sharding import PartitionSpec as P

ENTROPY = 0.05
HIGHEST_PREC = lax.Precision.HIGHEST


def from_everyone(shard, axis):
    peers = lax.axis_size(axis)
    return lax.all_to_all(
        jnp.broadcast_to(shard[None], (peers, *shard.shape)), axis, 0, 0, tiled=True
    )


def gathered_once(shard, axis):
    leaves = jax.tree.leaves(shard)
    order = sorted(range(len(leaves)), key=lambda k: -leaves[k].size)
    width = (1, *leaves[order[0]].shape)[-1]
    lines = [
        jnp.pad(leaves[k].reshape(-1), (0, -leaves[k].size % width)).reshape(-1, width)
        for k in order
    ]
    both, at, found = (from_everyone(jnp.concatenate(lines), axis), 0, {})
    for k, line in zip(order, lines):
        share = both[:, at : at + len(line)].reshape(len(both), -1)
        found[k] = share[:, : leaves[k].size].reshape(-1, *leaves[k].shape)
        at += len(line)
    numbers = iter(range(len(leaves)))
    return jax.tree.map(lambda _: found[next(numbers)], shard)


def combined_pairwise(pieces, combine):
    while len(jax.tree.leaves(pieces)[0]) > 1:
        pieces = jax.vmap(combine)(
            *(jax.tree.map(lambda part: part[side::2], pieces) for side in (0, 1))
        )
    return jax.tree.map(lambda part: part[0], pieces)


def joined_all(shard, axis, combine):
    pieces = gathered_once(shard, axis)
    return combined_pairwise(pieces, combine)


def once_a_type(shard, axis):
    leaves, found = (jax.tree.leaves(shard), {})
    for initial, a in enumerate(leaves):
        if initial not in found:
            alike = [k for k, b in enumerate(leaves) if b.dtype == a.dtype]
            got = (
                gathered_once([leaves[k] for k in alike], axis)
                if len(alike) > 1
                else [from_everyone(a, axis)]
            )
            for k, b in zip(alike, got):
                found[k] = b
    numbers = iter(range(len(leaves)))
    return jax.tree.map(lambda _: found[next(numbers)], shard)


def joined_all_2(shard, axis, combine):
    pieces = once_a_type(shard, axis)
    return combined_pairwise(pieces, combine)


def of_everyone(shard, axis):
    return from_everyone(shard, axis).max(axis=0)


def of_everyone_2(shard, axis):
    return from_everyone(shard, axis).sum(axis=0)


def combine_pairs(first, second):
    new_peak = jnp.maximum(first[0], second[0])
    total = first[1] * jnp.exp(first[0] - new_peak) + second[1] * jnp.exp(second[0] - new_peak)
    return (new_peak, total)


def on_device(noise_points, data_points, times, time_shift, weight_in, weight_out):
    count_row = lax.axis_size("row")
    count_col = lax.axis_size("col")
    rows_here = noise_points.shape[0]
    cols_here = data_points.shape[0]
    total_noise = rows_here * count_row
    total_data = cols_here * count_col
    width = noise_points.shape[1]
    noise_sq = jnp.sum(noise_points * noise_points, axis=1)
    data_sq = jnp.sum(data_points * data_points, axis=1)
    inner = jnp.dot(
        noise_points, data_points.T, precision=HIGHEST_PREC, preferred_element_type=jnp.float32
    )
    cost = (noise_sq[:, None] + data_sq[None, :] - 2.0 * inner) / width
    potential_g = jnp.zeros((cols_here,), jnp.float32)
    scores = (potential_g[None, :] - cost) / ENTROPY
    local_peak = jnp.max(scores, axis=1)
    local_total = jnp.sum(jnp.exp(scores - local_peak[:, None]), axis=1)
    row_peak, row_total = joined_all((local_peak, local_total), "col", combine_pairs)
    potential_f = -ENTROPY * (row_peak + jnp.log(row_total) - math.log(float(total_data)))
    scores = (potential_f[:, None] - cost) / ENTROPY
    local_peak = jnp.max(scores, axis=0)
    local_total = jnp.sum(jnp.exp(scores - local_peak[None, :]), axis=0)
    col_peak, col_total = joined_all_2((local_peak, local_total), "row", combine_pairs)
    potential_g = -ENTROPY * (col_peak + jnp.log(col_total) - math.log(float(total_noise)))
    scores = (potential_g[None, :] - cost) / ENTROPY
    final_peak = of_everyone(jnp.max(scores, axis=1), "col")
    weights = jnp.exp(scores - final_peak[:, None])
    numer = jnp.dot(
        weights, data_points, precision=HIGHEST_PREC, preferred_element_type=jnp.float32
    )
    denom = jnp.sum(weights, axis=1)
    numer_rows, denom_rows = (
        lax.psum_scatter(numer, "col", scatter_dimension=0, tiled=True),
        lax.psum_scatter(denom, "col", scatter_dimension=0, tiled=True),
    )
    target = numer_rows / denom_rows[:, None]
    share = rows_here // count_col
    anchor = lax.dynamic_slice_in_dim(noise_points, lax.axis_index("col") * share, share, 0)
    steps_each = times.shape[1]
    tvals = times[:, :, None]
    mixed = (
        ((1.0 - tvals) * anchor[:, None, :] + tvals * target[:, None, :])
        .reshape(share * steps_each, width)
        .astype(jnp.bfloat16)
    )
    velocity = jnp.broadcast_to((target - anchor)[:, None, :], (share, steps_each, width)).reshape(
        share * steps_each, width
    )
    hid_width = weight_in.shape[1]
    pre = (
        jnp.dot(mixed, weight_in, preferred_element_type=jnp.float32)
        + times.reshape(share * steps_each, 1) * time_shift[None, :]
    )
    hidden = jax.nn.silu(pre).astype(jnp.bfloat16)
    output = jnp.dot(hidden, weight_out, preferred_element_type=jnp.float32)
    predicted = output.astype(jnp.bfloat16)
    scale = 1.0 / math.sqrt(float(total_noise * steps_each))
    delta = ((output - velocity) * scale).astype(jnp.bfloat16)
    back = lax.dot_general(
        delta, weight_out, (((1,), (1,)), ((), ())), preferred_element_type=jnp.float32
    )
    sig = jax.nn.sigmoid(pre)
    delta_pre = (back * sig * (1.0 + pre * (1.0 - sig))).astype(jnp.bfloat16)
    contract = (((0,), (0,)), ((), ()))
    first = lax.dot_general(mixed, delta_pre, contract, preferred_element_type=jnp.float32)
    second = lax.dot_general(delta, hidden, contract, preferred_element_type=jnp.float32)
    part = lax.psum_scatter(
        jnp.concatenate([first, second], axis=1), "col", scatter_dimension=0, tiled=True
    )
    part = of_everyone_2(part, "row")
    summed = lax.all_gather(part, "col", axis=0, tiled=True)
    grad_in = summed[:, :hid_width]
    grad_out = summed[:, hid_width:].T
    return (predicted, grad_in, grad_out)


def solution(mesh):
    in_specs = (P("row", None), P("col", None), P(("row", "col"), None), P(), P(), P())
    out_specs = (P(("row", "col"), None), P(), P())
    return jax.shard_map(
        on_device, mesh=mesh, in_specs=in_specs, out_specs=out_specs, check_vma=False
    )
```

profile of v0, /device:TPU:1, one launch (start us, length us, event | category | flops | bytes accessed | tf_op | source)
XLA Modules:
  0.0 363.5 jit_solution(16436237428721453556)
XLA Ops:
  7.2 1.3 multiply_reduce_fusion.1
  8.5 4.2 %multiply_reduce_fusion = f32[4096]{0:T(1024)S(1)} fusion(f32[4096,512]{1,0:T(8,128)} %param.6), kind=kLoop, calls=%fused_computation.4 | loop fusion | flops 4190208 | bytes 8404992 | tf_op jit(solution)/shard_map/reduce_sum | solution.py:92
  12.7 1.6 copy-done.4
  14.3 7.9 %fusion.6 = (f32[4096]{0:T(1024)S(1)}, f32[4096,256]{0,1:T(8,128)S(1)}) fusion(f32[4096,512]{1,0:T(8,128)S(1)} %copy-done.4, f32[256,512]{1,0:T(8,128)S(1)} %copy-done.5, f32[256]{0:T(256)S(1)} %multiply_reduce_fusion.1, f32[4096]{0:T(1024)S(1)} %multiply_reduce_fusion), kind=kOutput, calls=%fused_computation.22 | convolution fusion | flops 6449786880 | bytes 13140992 | tf_op jit(solution)/shard_map/dot_general | solution.py:94
  22.2 2.0 copy-done.2
  24.1 0.8 exponential_reduce_fusion.1
  25.2 17.2 %all_to_all.21 = f32[16,2,4096]{2,1,0:T(2,128)S(1)} all-to-all(f32[16,2,4096]{2,1,0:T(2,128)S(1)} %broadcast_in_dim.10), channel_id=1, replica_groups=mesh['row'=8,'col'=16] {'col'}, dimensions={0} | all-to-all | bytes 1048576 | tf_op jit(solution)/shard_map/all_to_all | solution.py:14
  42.4 0.5 fusion.40
  45.0 2.9 fusion.7
  48.3 0.9 exponential_reduce_fusion
  49.2 12.7 %all_to_all.22 = f32[8,2,256]{2,1,0:T(2,128)S(1)} all-to-all(f32[8,2,256]{2,1,0:T(2,128)S(1)} %broadcast_in_dim.11), channel_id=1, replica_groups=mesh['row'=8,'col'=16] {'row'}, dimensions={0} | all-to-all | bytes 32768 | tf_op jit(solution)/shard_map/all_to_all | solution.py:14
  62.2 2.8 fusion.8
  65.2 12.4 %all_to_all.23 = f32[16,1,4096]{2,1,0:T(1,128)S(1)} all-to-all(f32[16,1,4096]{2,1,0:T(1,128)S(1)} %broadcast_in_dim.12), channel_id=1, replica_groups=mesh['row'=8,'col'=16] {'col'}, dimensions={0} | all-to-all | bytes 524288 | tf_op jit(solution)/shard_map/all_to_all | solution.py:14
  77.7 11.1 %fusion.10 = f32[4096,512]{1,0:T(8,128)} fusion(f32[256,512]{1,0:T(8,128)S(1)} %copy-done.5, f32[4096,256]{0,1:T(8,128)} %copy-done.2, f32[4096]{0:T(1024)S(1)} %reduce_max.39, f32[256]{0:T(256)S(1)} %bitcast.63), kind=kOutput, calls=%fused_computation.26 | convolution fusion | flops 6445596672 | bytes 13124608 | tf_op jit(solution)/shard_map/dot_general | solution.py:112
  88.9 0.6 copy-done.12
  90.0 0.6 dynamic-slice
  91.3 3.4 fusion.9
  94.7 51.4 %all-reduce = f32[4096]{0:T(1024)S(1)} all-reduce(f32[4096]{0:T(1024)S(1)} %fusion.9), channel_id=3, replica_groups=mesh['row'=8,'col'=16] {'col'}, use_global_device_ids=true, to_apply=%region_10.11.clone | all-reduce | flops 4096 | bytes 32768
  146.2 35.4 %reduce-scatter.3.cloned.1.call-done = f32[256,512]{1,0:T(8,128)} async-done(((f32[4096,512]{1,0:T(8,128)}), f32[256,512]{1,0:T(8,128)}) %reduce-scatter.3.cloned.1.call-update) | async-done | bytes 524304 | tf_op jit(solution)/shard_map/reduce_scatter | solution.py:117
  181.6 1.3 fusion.39
  183.0 6.1 %multiply_convert_fusion.1 = (bf16[2048,1024]{1,0:T(8,128)(2,1)S(1)}, f32[2048,1024]{1,0:T(8,128)}) fusion(f32[1024]{0:T(1024)S(1)} %copy-done.14, f32[2048]{0:T(1024)S(1)} %mul.151, bf16[512,1024]{1,0:T(8,128)(2,1)S(1)} %copy-done, f32[256,512]{1,0:T(8,128)S(1)} %get-tuple-element.20, f32[256,512]{1,0:T(8,128)S(1)} %get-tuple-element.19, f32[2048]{0:T(1024)S(1)} %mul.145), kind=kOutput, calls=%fused_computation.1 | convolution fusion | flops 2166358016 | bytes 14700544 | tf_op jit(solution)/shard_map/dot_general | solution.py:135
  189.1 3.7 %fusion.42 = (bf16[2048,512]{1,0:T(8,128)(2,1)}, f32[2048,512]{1,0:T(8,128)S(1)}) fusion(bf16[2048,1024]{1,0:T(8,128)(2,1)S(1)} %get-tuple-element.39, bf16[1024,512]{1,0:T(8,128)(2,1)S(1)} %copy-done.13), kind=kOutput, calls=%fused_computation.76 | convolution fusion | flops 2148532224 | bytes 11534336 | tf_op jit(solution)/shard_map/dot_general | solution.py:139
  192.8 2.4 fusion.26
  195.2 12.4 %fusion.11 = f32[512,1024]{1,0:T(8,128)} fusion(f32[256,512]{1,0:T(8,128)S(1)} %copy-done.11, f32[2048]{0:T(1024)S(1)} %mul.151, f32[256,512]{1,0:T(8,128)S(1)} %copy-done.9, f32[2048]{0:T(1024)S(1)} %mul.145, f32[2048,1024]{1,0:T(8,128)} %get-tuple-element.40, bf16[1024,512]{1,0:T(8,128)(2,1)} %param.11, f32[1024]{0:T(1024)S(1)} %copy-done.14, ...), kind=kOutput, calls=%fused_computation.27 | convolution fusion | flops 4325376000 | bytes 17321984 | tf_op jit(solution)/shard_map/dot_general | solution.py:149
  207.7 3.9 %pad_maximum_fusion = f32[512,2048]{1,0:T(8,128)} fusion(f32[512,1024]{1,0:T(8,128)S(1)} %fusion.26, f32[512,1024]{1,0:T(8,128)} %fusion.11), kind=kLoop, calls=%fused_computation.8 | loop fusion | flops 1048576 | bytes 8388608 | tf_op jit(solution)/shard_map/concatenate | solution.py:152
  211.6 68.8 %reduce-scatter.5.cloned.1.call-done = f32[32,2048]{1,0:T(8,128)} async-done(((f32[512,2048]{1,0:T(8,128)}), f32[32,2048]{1,0:T(8,128)}) %reduce-scatter.5.cloned.1.call-update) | async-done | bytes 262160 | tf_op jit(solution)/shard_map/reduce_scatter | solution.py:151
  280.4 1.2 broadcast_in_dim.14
  281.6 30.8 %all_to_all.24 = f32[8,32,2048]{2,1,0:T(8,128)S(1)} all-to-all(f32[8,32,2048]{2,1,0:T(8,128)S(1)} %broadcast_in_dim.14), channel_id=1, replica_groups=mesh['row'=8,'col'=16] {'row'}, dimensions={0} | all-to-all | bytes 4194304 | tf_op jit(solution)/shard_map/all_to_all | solution.py:14
  312.5 0.8 reduce_sum.59
  313.3 37.8 %all-gather.2.cloned.1.call-done = f32[512,2048]{1,0:T(8,128)} async-done(((f32[32,2048]{1,0:T(8,128)}), f32[512,2048]{1,0:T(8,128)}) %all-gather.2.cloned.1.call-update) | async-done | bytes 4194320 | tf_op jit(solution)/shard_map/all_gather | solution.py:155
  351.1 4.1 %slice_bitcast_fusion = (f32[1024,512]{0,1:T(8,128)S(1)}, f32[512,1024]{1,0:T(8,128)}) fusion(f32[512,2048]{1,0:T(8,128)} %all-gather.2.cloned.1.call-done), kind=kLoop, calls=%fused_computation.29 | loop fusion | bytes 8388608 | tf_op jit(solution)/shard_map/transpose | solution.py:157
  355.2 1.8 copy.32
  (78 shorter events, 3.9 us)
Async XLA Ops:
  7.2 175.8 %copy-start = (bf16[512,1024]{1,0:T(8,128)(2,1)S(1)}, bf16[512,1024]{1,0:T(8,128)(2,1)}, u32[]{:S(2)}) copy-start(bf16[512,1024]{1,0:T(8,128)(2,1)} %param.10) | copy-start | bytes 3145732
  7.2 174.4 %reduce-scatter.3.cloned.1.call-start = ((), (), s32[]{:S(2)}) async-start(), calls=%async_computation.6 | async-start | bytes 8912896 | tf_op jit(solution)/shard_map/reduce_scatter | solution.py:117
  7.2 5.5 %copy-start.5 = (f32[256,512]{1,0:T(8,128)S(1)}, f32[256,512]{1,0:T(8,128)}, u32[]{:S(2)}) copy-start(f32[256,512]{1,0:T(8,128)} %param.7) | copy-start | bytes 1572868
  8.5 5.8 %copy-start.4 = (f32[4096,512]{1,0:T(8,128)S(1)}, f32[4096,512]{1,0:T(8,128)}, u32[]{:S(2)}) copy-start(f32[4096,512]{1,0:T(8,128)} %param.6) | copy-start | bytes 25165828
  22.2 2.0 copy-start.2
  44.8 3.5 copy-start.3
  88.8 0.7 copy-start.12
  88.8 1.2 copy-start.15
  88.9 94.1 %copy-start.14 = (f32[1024]{0:T(1024)S(1)}, f32[1024]{0:T(1024)}, u32[]{:S(2)}) copy-start(f32[1024]{0:T(1024)} %param.9) | copy-start | bytes 12292
  88.9 191.6 %reduce-scatter.5.cloned.1.call-start = ((), (), s32[]{:S(2)}) async-start(), calls=%async_computation.7 | async-start | bytes 4456448 | tf_op jit(solution)/shard_map/reduce_scatter | solution.py:151
  182.9 6.2 %copy-start.8 = (f32[256,512]{1,0:T(8,128)}, f32[256,512]{1,0:T(8,128)S(1)}, u32[]{:S(2)}) copy-start(f32[256,512]{1,0:T(8,128)S(1)} %get-tuple-element.19) | copy-start | bytes 1572868
  182.9 6.2 %copy-start.10 = (f32[256,512]{1,0:T(8,128)}, f32[256,512]{1,0:T(8,128)S(1)}, u32[]{:S(2)}) copy-start(f32[256,512]{1,0:T(8,128)S(1)} %get-tuple-element.20) | copy-start | bytes 1572868
  182.9 9.9 %copy-start.7 = (f32[256,512]{1,0:T(8,128)}, f32[256,512]{1,0:T(8,128)S(1)}, u32[]{:S(2)}) copy-start(f32[256,512]{1,0:T(8,128)S(1)} %get-tuple-element.18) | copy-start | bytes 1572868
  183.0 6.2 %copy-start.13 = (bf16[1024,512]{1,0:T(8,128)(2,1)S(1)}, bf16[1024,512]{1,0:T(8,128)(2,1)}, u32[]{:S(2)}) copy-start(bf16[1024,512]{1,0:T(8,128)(2,1)} %param.11) | copy-start | bytes 3145732
  192.8 2.4 copy-start.6
  192.8 2.4 copy-start.9
  192.8 2.4 copy-start.11
  211.6 139.5 %all-gather.2.cloned.1.call-start = ((), (), s32[]{:S(2)}) async-start(), calls=%async_computation.8 | async-start | bytes 4456448 | tf_op jit(solution)/shard_map/all_gather | solution.py:155
  351.1 5.9 %copy-start.1 = (bf16[512,1024]{1,0:T(8,128)(2,1)S(1)}, bf16[512,1024]{1,0:T(8,128)(2,1)}, u32[]{:S(2)}) copy-start(bf16[512,1024]{1,0:T(8,128)(2,1)} %param.10) | copy-start | bytes 3145732
Sparse Core Ops, SparseCore 0:
  89.0 92.5 reduce-scatter.2
  211.7 68.6 reduce-scatter.4
  313.4 37.6 all-gather.1
where the time goes:
time: 364 us
  waiting for transfers between devices  142 us (39%)
  blocking collectives  125 us (34%)
  matrix products  43.6 us (12%)
  other arithmetic  22.9 us (6%)
  local copies, waits for them, and re-layouts  15.6 us (4%)
  between operations  14.8 us (4%)
    all_to_all x4, blocking collectives, from_everyone(): lax.all_to_all(jnp.broadcast_to(shard[None], (peers, *shard.shape)), axis...  73.1 us
    reduce_scatter x1, waiting for transfers between devices, on_device(): lax.psum_scatter(jnp.concatenate([first, second], axis=1), 'col', scatter...  68.8 us
    unnamed x1, blocking collectives  51.4 us
    all_gather x1, waiting for transfers between devices, on_device(): summed = lax.all_gather(part, 'col', axis=0, tiled=True)  37.8 us
    reduce_scatter x1, waiting for transfers between devices, on_device(): lax.psum_scatter(numer, 'col', scatter_dimension=0, tiled=True)  35.4 us
    dot_general x1, matrix products, on_device(): lax.dot_general(mixed, delta_pre, contract, preferred_element_type=jnp.fl...  12.4 us
    dot_general x1, matrix products, on_device(): jnp.dot(weights, data_points, precision=HIGHEST_PREC, preferred_element_t...  11.1 us
    dot_general x1, matrix products, on_device(): jnp.dot(noise_points, data_points.T, precision=HIGHEST_PREC, preferred_el...  7.89 us
  transfers between devices with their start and end apart: 3, of which 3 were waited for; matrix products, arithmetic and copies ran while one was open for 1% of the time, Pallas kernels for 0%

commit v1 on v0

v1 whole, which is shorter than its diff:
```python
import functools
import math

import jax
import jax.numpy as jnp
from jax import lax
from jax.experimental import pallas as pl
from jax.experimental.pallas import tpu as pltpu
from jax.sharding import PartitionSpec as P

ENTROPY = 0.05
HIGH_PREC = lax.Precision.HIGH
MESH = pl.DeviceIdType.MESH
VMEM_CAP = 60 * 1024 * 1024


class Place:
    def __init__(self):
        row, col = lax.axis_index("row"), lax.axis_index("col")
        self.core = col % 2
        x = (row % 2) * 2 + (col // 2) % 2
        y = row // 2
        z = col // 4
        self.bits = []
        for pos in (x, y, z):
            self.bits.append(((pos + pos // 2) % 2, pos // 2))
        (xa, xb), (ya, yb), (za, zb) = self.bits
        self.groups = ((xa, ya), (yb, za), (zb, xb))
        self.q = tuple(u * 2 + v for u, v in self.groups)
        self.row, self.col = row, col

    def partner(self, group, flip):
        hi, lo = flip // 2, flip % 2
        groups = [list(g) for g in self.groups]
        if hi:
            groups[group][0] = 1 - groups[group][0]
        if lo:
            groups[group][1] = 1 - groups[group][1]
        (xa, ya), (yb, za), (zb, xb) = groups
        x, y, z = ((2 * b + (a + b) % 2) for a, b in ((xa, xb), (ya, yb), (za, zb)))
        return (y * 2 + x // 2, z * 4 + (x % 2) * 2 + self.core)

    def other_core(self):
        return (self.row, self.col + 1 - 2 * self.core)

    def flipped(self, group, flip):
        hi, lo = self.groups[group]
        if flip // 2:
            hi = 1 - hi
        if flip % 2:
            lo = 1 - lo
        return hi * 2 + lo


def meet(place):
    barrier = pltpu.get_barrier_semaphore()
    pl.semaphore_signal(barrier, inc=1, device_id=place.other_core(), device_id_type=MESH)
    for group in range(3):
        for flip in (1, 2, 3):
            pl.semaphore_signal(
                barrier, inc=1, device_id=place.partner(group, flip), device_id_type=MESH
            )
    pl.semaphore_wait(barrier, 10)


def at_groups(turn, first=None, second=None, third=None):
    found = [slice(None)] * 3
    for k, value in enumerate((first, second, third)):
        if value is not None:
            found[(turn + k) % 3] = value
    return tuple(found)


def gather_phases(place, out, pieces, sems, base):
    send, recv = sems
    mine = out.at[place.core]
    started = []

    def copy(src, dst, number, device):
        made = pltpu.make_async_remote_copy(
            src_ref=src, dst_ref=dst, send_sem=send.at[number], recv_sem=recv.at[number],
            device_id=device, device_id_type=MESH,
        )
        made.start()
        started.append(made)
        return made

    def spot(piece, *values):
        rows, cols, turn = piece
        return mine.at[(*at_groups(turn, *values), rows, cols)]

    waiting = [[] for _ in pieces]
    for phase in range(3):
        for n, piece in enumerate(pieces):
            turn = piece[2]
            q = [place.q[(turn + k) % 3] for k in range(3)]
            for made in waiting[n]:
                made.wait_recv()
            waiting[n] = []
            held = (q, q[:2], q[:1])[phase]
            group = (turn + 2 - phase) % 3
            block = spot(piece, *held)
            for flip in (1, 2, 3):
                number = base + (n * 3 + phase) * 3 + flip - 1
                waiting[n].append(copy(block, block, number, place.partner(group, flip)))
    first = base + 9 * len(pieces)
    across = []
    for n, piece in enumerate(pieces):
        turn = piece[2]
        own = place.q[turn]
        block = spot(piece, own)
        across.append(copy(block, block, first + 4 * n, place.other_core()))
    for n, piece in enumerate(pieces):
        turn = piece[2]
        for flip in (1, 2, 3):
            waiting[n][flip - 1].wait_recv()
            block = spot(piece, place.flipped(turn, flip))
            across.append(copy(block, block, first + 4 * n + flip, place.other_core()))
    for made in across:
        made.wait_recv()
    for made in started:
        made.wait_send()


def data_kernel(pieces, data_ref, out_ref, local_sem, send_sem, recv_sem):
    place = Place()
    rows = out_ref.shape[4]
    start = pl.multiple_of(place.row * rows, rows)
    unit = out_ref.at[(place.core, *place.q)]
    bring = pltpu.make_async_copy(data_ref.at[pl.ds(start, rows)], unit, local_sem)
    bring.start()
    meet(place)
    bring.wait()
    gather_phases(place, out_ref, pieces, (send_sem, recv_sem), 0)


def gather_data(data_points):
    count, width = data_points.shape
    peers = lax.axis_size("row")
    rows = count // peers
    quarter, tile = rows // 4, width // 4
    every = slice(None)
    last = slice(3 * quarter, rows)
    pieces = (
        (slice(0, quarter), every, 0),
        (slice(quarter, 2 * quarter), every, 1),
        (slice(2 * quarter, 3 * quarter), every, 2),
        (last, slice(0, tile), 0),
        (last, slice(tile, 2 * tile), 1),
        (last, slice(2 * tile, width), 2),
    )
    copies = 13 * len(pieces)
    out = pl.pallas_call(
        functools.partial(data_kernel, pieces),
        out_shape=jax.ShapeDtypeStruct((2, 4, 4, 4, rows, width), data_points.dtype),
        in_specs=[pl.BlockSpec(memory_space=pl.ANY)],
        out_specs=pl.BlockSpec(memory_space=pltpu.VMEM),
        scratch_shapes=[
            pltpu.SemaphoreType.DMA,
            pltpu.SemaphoreType.DMA((copies,)),
            pltpu.SemaphoreType.DMA((copies,)),
        ],
        compiler_params=pltpu.CompilerParams(
            collective_id=1, has_side_effects=True, vmem_limit_bytes=VMEM_CAP
        ),
        name="gather_data",
    )(data_points)
    return out.reshape(-1, width)


def join_pairs(first, second):
    peak = jnp.maximum(first[0], second[0])
    total = first[1] * jnp.exp(first[0] - peak) + second[1] * jnp.exp(second[0] - peak)
    return peak, total


def columns_kernel(in_ref, out_ref, held, slots, from_core, send_sem, recv_sem):
    place = Place()
    core = place.core
    meet(place)

    def copy(src, dst, number, device):
        made = pltpu.make_async_remote_copy(
            src_ref=src, dst_ref=dst, send_sem=send_sem.at[number], recv_sem=recv_sem.at[number],
            device_id=device, device_id_type=MESH,
        )
        made.start()
        return made

    other = 1 - core
    started = [copy(in_ref.at[other], from_core, 0, place.other_core())]
    started[0].wait_recv()
    own = in_ref[core]
    got = from_core[...]
    pair = join_pairs((own[0], own[1]), (got[0], got[1]))
    for group in range(3):
        held[group, 0] = pair[0]
        held[group, 1] = pair[1]
        now = [
            copy(held.at[group], slots.at[group, flip - 1], 3 * group + flip,
                 place.partner(group, flip))
            for flip in (1, 2, 3)
        ]
        started += now
        for flip in (1, 2, 3):
            now[flip - 1].wait_recv()
        new_peak = pair[0]
        for k in range(3):
            new_peak = jnp.maximum(new_peak, slots[group, k, 0])
        total = pair[1] * jnp.exp(pair[0] - new_peak)
        for k in range(3):
            total = total + slots[group, k, 1] * jnp.exp(slots[group, k, 0] - new_peak)
        pair = (new_peak, total)
    out_ref[core, 0] = pair[0]
    out_ref[core, 1] = pair[1]
    final = copy(out_ref.at[core], out_ref.at[core], 10, place.other_core())
    started.append(final)
    final.wait_recv()
    for made in started:
        made.wait_send()


def join_columns(pairs):
    shape = pairs.shape
    return pl.pallas_call(
        columns_kernel,
        out_shape=jax.ShapeDtypeStruct(shape, pairs.dtype),
        in_specs=[pl.BlockSpec(memory_space=pltpu.VMEM)],
        out_specs=pl.BlockSpec(memory_space=pltpu.VMEM),
        scratch_shapes=[
            pltpu.VMEM((3, *shape[1:]), jnp.float32),
            pltpu.VMEM((3, 3, *shape[1:]), jnp.float32),
            pltpu.VMEM(shape[1:], jnp.float32),
            pltpu.SemaphoreType.DMA((11,)),
            pltpu.SemaphoreType.DMA((11,)),
        ],
        compiler_params=pltpu.CompilerParams(collective_id=2, has_side_effects=True),
        name="join_columns",
    )(pairs)


def grads_kernel(pieces, in_ref, out_ref, acc, from_core, slot_0, slot_1, slot_2, send_sem, recv_sem):
    place = Place()
    core = place.core
    meet(place)
    count = len(pieces)

    def copy(src, dst, number, device):
        made = pltpu.make_async_remote_copy(
            src_ref=src, dst_ref=dst, send_sem=send_sem.at[number], recv_sem=recv_sem.at[number],
            device_id=device, device_id_type=MESH,
        )
        made.start()
        return made

    every = slice(None)
    other = 1 - core
    started = []
    first = []
    for n, (rows, cols, turn) in enumerate(pieces):
        made = copy(in_ref.at[other, :, :, :, :, cols], from_core.at[:, :, :, :, cols], n,
                    place.other_core())
        first.append(made)
    started += first
    base = count
    waiting = [[] for _ in pieces]
    for n, (rows, cols, turn) in enumerate(pieces):
        first[n].wait_recv()

        @pl.loop(0, 16)
        def _(i, cols=cols):
            a, b = i // 4, i % 4
            acc[a, b, :, :, cols] = in_ref[core, a, b, :, :, cols] + from_core[a, b, :, :, cols]

        for flip in (1, 2, 3):
            src = acc.at[(*at_groups(turn, place.flipped(turn, flip)), every, cols)]
            waiting[n].append(
                copy(src, slot_0.at[n, flip - 1, :, :, :, 0 : cols.stop - cols.start],
                     base + n * 3 + flip - 1, place.partner(turn, flip))
            )
    base += 3 * count
    for phase in (1, 2):
        for n, (rows, cols, turn) in enumerate(pieces):
            wide = slice(0, cols.stop - cols.start)
            q = [place.q[(turn + k) % 3] for k in range(3)]
            for made in waiting[n]:
                made.wait_recv()
            started += waiting[n]
            waiting[n] = []
            group = (turn + phase) % 3
            if phase == 1:
                lead = at_groups(turn, q[0])
                acc[(*lead, every, cols)] = (
                    (acc[(*lead, every, cols)] + slot_0[n, 0, :, :, :, wide])
                    + (slot_0[n, 1, :, :, :, wide] + slot_0[n, 2, :, :, :, wide])
                )
            else:
                lead = at_groups(turn, q[0], q[1])
                acc[(*lead, every, cols)] = (
                    (acc[(*lead, every, cols)] + slot_1[n, 0, :, :, wide])
                    + (slot_1[n, 1, :, :, wide] + slot_1[n, 2, :, :, wide])
                )
            for flip in (1, 2, 3):
                theirs = place.flipped(group, flip)
                if phase == 1:
                    src = acc.at[(*at_groups(turn, q[0], theirs), every, cols)]
                    dst = slot_1.at[n, flip - 1, :, :, wide]
                else:
                    src = acc.at[(*at_groups(turn, q[0], q[1], theirs), every, cols)]
                    dst = slot_2.at[n, flip - 1, :, wide]
                waiting[n].append(
                    copy(src, dst, base + n * 3 + flip - 1, place.partner(group, flip))
                )
        base += 3 * count
    for n, (rows, cols, turn) in enumerate(pieces):
        wide = slice(0, cols.stop - cols.start)
        for made in waiting[n]:
            made.wait_recv()
        started += waiting[n]
        out_ref[(core, *place.q, every, cols)] = (
            (acc[(*place.q, every, cols)] + slot_2[n, 0, :, wide])
            + (slot_2[n, 1, :, wide] + slot_2[n, 2, :, wide])
        )
    gather_phases(place, out_ref, pieces, (send_sem, recv_sem), base)
    for made in started:
        made.wait_send()


def sum_grads(grads):
    shape = grads.shape
    width = shape[-1]
    share = 128 * -(-width // 384)
    every = slice(None)
    pieces = (
        (every, slice(0, share), 0),
        (every, slice(share, 2 * share), 1),
        (every, slice(2 * share, width), 2),
    )
    copies = (1 + 9 + 13) * len(pieces)
    f32 = jnp.float32
    return pl.pallas_call(
        functools.partial(grads_kernel, pieces),
        out_shape=jax.ShapeDtypeStruct(shape, f32),
        in_specs=[pl.BlockSpec(memory_space=pltpu.VMEM)],
        out_specs=pl.BlockSpec(memory_space=pltpu.VMEM),
        scratch_shapes=[
            pltpu.VMEM(shape[1:], f32),
            pltpu.VMEM(shape[1:], f32),
            pltpu.VMEM((3, 3, 4, 4, 8, share), f32),
            pltpu.VMEM((3, 3, 4, 8, share), f32),
            pltpu.VMEM((3, 3, 8, share), f32),
            pltpu.SemaphoreType.DMA((copies,)),
            pltpu.SemaphoreType.DMA((copies,)),
        ],
        compiler_params=pltpu.CompilerParams(
            collective_id=3, has_side_effects=True, vmem_limit_bytes=VMEM_CAP
        ),
        name="sum_grads",
    )(grads)


def on_device(noise_points, data_points, times, time_shift, weight_in, weight_out):
    count_row = lax.axis_size("row")
    count_col = lax.axis_size("col")
    rows_here = noise_points.shape[0]
    total_noise = rows_here * count_row
    total_data = data_points.shape[0] * count_col
    width = noise_points.shape[1]
    share = rows_here // count_col
    steps_each = times.shape[1]

    data_all = gather_data(data_points)
    anchor = lax.dynamic_slice_in_dim(noise_points, lax.axis_index("col") * share, share, 0)
    noise_sq = jnp.sum(anchor * anchor, axis=1)
    data_sq = jnp.sum(data_all * data_all, axis=1)
    inner = lax.dot_general(
        anchor, data_all, (((1,), (1,)), ((), ())), precision=HIGH_PREC,
        preferred_element_type=jnp.float32,
    )
    cost = (noise_sq[:, None] + data_sq[None, :] - 2.0 * inner) / width
    scores = -cost / ENTROPY
    row_peak = jnp.max(scores, axis=1)
    row_total = jnp.sum(jnp.exp(scores - row_peak[:, None]), axis=1)
    potential_f = -ENTROPY * (row_peak + jnp.log(row_total) - math.log(float(total_data)))
    scores = (potential_f[:, None] - cost) / ENTROPY
    local_peak = jnp.max(scores, axis=0)
    local_total = jnp.sum(jnp.exp(scores - local_peak[None, :]), axis=0)
    pairs = jnp.stack(
        [local_peak.reshape(2, -1, 128), local_total.reshape(2, -1, 128)], axis=1
    )
    joined = join_columns(pairs)
    col_peak, col_total = joined[:, 0].reshape(-1), joined[:, 1].reshape(-1)
    potential_g = -ENTROPY * (col_peak + jnp.log(col_total) - math.log(float(total_noise)))
    scores = (potential_g[None, :] - cost) / ENTROPY
    final_peak = jnp.max(scores, axis=1)
    weights = jnp.exp(scores - final_peak[:, None])
    numer = jnp.dot(weights, data_all, precision=HIGH_PREC, preferred_element_type=jnp.float32)
    target = numer / jnp.sum(weights, axis=1)[:, None]

    tvals = times[:, :, None]
    mixed = (
        ((1.0 - tvals) * anchor[:, None, :] + tvals * target[:, None, :])
        .reshape(share * steps_each, width)
        .astype(jnp.bfloat16)
    )
    velocity = jnp.broadcast_to((target - anchor)[:, None, :], (share, steps_each, width)).reshape(
        share * steps_each, width
    )
    hid_width = weight_in.shape[1]
    pre = (
        jnp.dot(mixed, weight_in, preferred_element_type=jnp.float32)
        + times.reshape(share * steps_each, 1) * time_shift[None, :]
    )
    hidden = jax.nn.silu(pre).astype(jnp.bfloat16)
    output = jnp.dot(hidden, weight_out, preferred_element_type=jnp.float32)
    predicted = output.astype(jnp.bfloat16)
    scale = 1.0 / math.sqrt(float(total_noise * steps_each))
    delta = ((output - velocity) * scale).astype(jnp.bfloat16)
    back = lax.dot_general(
        delta, weight_out, (((1,), (1,)), ((), ())), preferred_element_type=jnp.float32
    )
    sig = jax.nn.sigmoid(pre)
    delta_pre = (back * sig * (1.0 + pre * (1.0 - sig))).astype(jnp.bfloat16)
    contract = (((0,), (0,)), ((), ()))
    first = lax.dot_general(mixed, delta_pre, contract, preferred_element_type=jnp.float32)
    second = lax.dot_general(hidden, delta, contract, preferred_element_type=jnp.float32)
    halves = hid_width // width
    second = jnp.concatenate(
        [second[k * width : (k + 1) * width] for k in range(halves)], axis=1
    )
    grads = jnp.stack([first, second]).reshape(2, 4, 4, 4, width // 64, hid_width)
    summed = sum_grads(grads).reshape(2, width, hid_width)
    grad_in = summed[0]
    grad_out = jnp.concatenate(
        [summed[1][:, k * width : (k + 1) * width] for k in range(halves)], axis=0
    )
    return (predicted, grad_in, grad_out)


def solution(mesh):
    in_specs = (P("row", None), P("col", None), P(("row", "col"), None), P(), P(), P())
    out_specs = (P(("row", "col"), None), P(), P())
    return jax.shard_map(
        on_device, mesh=mesh, in_specs=in_specs, out_specs=out_specs, check_vma=False
    )
```

time: 364 us -> 186 us (0.51)
  waiting for transfers between devices: 142 us -> 0 us
  blocking collectives: 125 us -> 0 us
  Pallas kernels: 0 us -> 111 us
  between operations: 14.8 us -> 0.84 us
  matrix products: 43.6 us -> 39 us
    pallas_call x0 -> x3, Pallas kernels: none -> 111 us  [the longest x1 51.9 us: sum_grads(): pl.pallas_call(functools.partial(grads_kernel, pieces), out_shape=jax.Sha...]
    reduce_scatter x2 -> x0, waiting for transfers between devices: 104 us -> none  [the longest x1 68.8 us: on_device(): lax.psum_scatter(jnp.concatenate([first, second], axis=1), 'col', scatter...]
    all_to_all x4 -> x0, blocking collectives: 73.1 us -> none  [from_everyone(): lax.all_to_all(jnp.broadcast_to(shard[None], (peers, *shard.shape)), axis...]
    unnamed x1 -> x0, blocking collectives: 51.4 us -> none
    all_gather x1 -> x0, waiting for transfers between devices: 37.8 us -> none  [on_device(): summed = lax.all_gather(part, 'col', axis=0, tiled=True)]
    unnamed x38 -> x23, local copies, waits for them, and re-layouts: 7.22 us -> 1.46 us
    dot_general x3, matrix products: 21.4 us -> 16.5 us  [the longest x1 7.58 us: on_device(): jnp.dot(weights, data_all, precision=HIGH_PREC, preferred_element_type=jn...]
    another operation x0 -> x2, other arithmetic: none -> 4.57 us  [the longest x1 3.96 us: on_device(): jnp.stack([first, second]).reshape(2, 4, 4, 4, width // 64, hid_width)]
  transfers between devices with their start and end apart: 3 -> 0, of which waited for: 3 -> 0; matrix products, arithmetic and copies ran while one was open for 1% -> 0% of each run, Pallas kernels for 0% -> 0%
where the time goes in v1:
time: 186 us
  Pallas kernels  111 us (60%)
  matrix products  39 us (21%)
  other arithmetic  21.6 us (12%)
  local copies, waits for them, and re-layouts  13.1 us (7%)
    pallas_call x1, Pallas kernels, sum_grads(): pl.pallas_call(functools.partial(grads_kernel, pieces), out_shape=jax.Sha...  51.9 us
    pallas_call x1, Pallas kernels, gather_data(): pl.pallas_call(functools.partial(data_kernel, pieces), out_shape=jax.Shap...  42.3 us
    pallas_call x1, Pallas kernels, join_columns(): pl.pallas_call(columns_kernel, out_shape=jax.ShapeDtypeStruct(shape, pair...  17 us
    dot_general x1, matrix products, on_device(): lax.dot_general(mixed, delta_pre, contract, preferred_element_type=jnp.fl...  12.6 us
    dot_general x1, matrix products, on_device(): jnp.dot(weights, data_all, precision=HIGH_PREC, preferred_element_type=jn...  7.58 us
    dot_general x1, matrix products, on_device(): lax.dot_general(anchor, data_all, (((1,), (1,)), ((), ())), precision=HIG...  6.46 us
    dot_general x1, matrix products, on_device(): jnp.dot(mixed, weight_in, preferred_element_type=jnp.float32)  6.13 us
    slice x2, local copies, waits for them, and re-layouts, on_device(): summed[1][:, k * width:(k + 1) * width]  4.17 us

profile of v1, /device:TPU:1, one launch (start us, length us, event | category | flops | bytes accessed | tf_op | source)
XLA Modules:
  0.0 185.7 jit_solution(4476988478457305740)
XLA Ops:
  0.6 0.9 copy.17
  1.6 0.1 mul.113
  1.7 1.2 multiply_reduce_fusion.1
  2.8 42.3 %gather_data.1 = f32[2,4,4,4,32,512]{5,4,3,2,1,0:T(8,128)} custom-call(f32[256,512]{1,0:T(8,128)} %data_ref.1), custom_call_target="tpu_custom_call" | custom-call | tf_op jit(solution)/shard_map/gather_data/pallas_call | solution.py:153
  45.2 4.1 %multiply_reduce_fusion = f32[2,4,4,4,32]{4,3,2,1,0:T(4,128)S(1)} fusion(f32[2,4,4,4,32,512]{5,4,3,2,1,0:T(8,128)} %gather_data.1), kind=kLoop, calls=%fused_computation.4 | loop fusion | flops 4190208 | bytes 8404992 | tf_op jit(solution)/shard_map/reduce_sum | solution.py:375
  49.4 6.5 %fusion.11 = (f32[256]{0:T(256)S(1)}, f32[256,4096]{1,0:T(8,128)S(1)}) fusion(f32[256,512]{1,0:T(8,128)S(1)} %get-tuple-element.4, f32[4096,512]{1,0:T(8,128)} %bitcast.57, f32[4096]{0:T(1024)S(1)} %add.61, f32[256]{0:T(256)S(1)} %get-tuple-element.3), kind=kOutput, calls=%fused_computation.27 | convolution fusion | flops 3228565248 | bytes 13125632 | tf_op jit(solution)/shard_map/dot_general | solution.py:376
  55.8 0.8 exponential_reduce_fusion.1
  56.7 0.6 fusion.12
  57.3 0.5 copy-done.2
  57.8 0.9 exponential_reduce_fusion
  58.7 0.6 pad_maximum_fusion.3.in_ref
  59.3 17.0 %join_columns.1 = f32[2,2,16,128]{3,2,1,0:T(8,128)} custom-call(f32[2,2,16,128]{3,2,1,0:T(8,128)} %pad_maximum_fusion.3.in_ref), custom_call_target="tpu_custom_call" | custom-call | tf_op jit(solution)/shard_map/join_columns/pallas_call | solution.py:225
  76.4 0.9 add_multiply_fusion
  77.3 2.9 %fusion.13 = f32[256]{0:T(256)S(1)} fusion(f32[256,4096]{1,0:T(8,128)} %copy-done.2, f32[4096]{0:T(1024)S(1)} %bitcast.63), kind=kLoop, calls=%fused_computation.29 | loop fusion | flops 3145472 | bytes 4211712 | tf_op jit(solution)/shard_map/reduce_max | solution.py:395
  80.2 0.9 fusion.14
  81.2 7.6 %fusion.43 = (f32[256,512]{1,0:T(8,128)S(1)}, f32[256,512]{1,0:T(8,128)S(1)}) fusion(f32[256,512]{1,0:T(8,128)S(1)} %get-tuple-element.4, f32[256]{0:T(256)S(1)} %fusion.14, f32[4096,512]{1,0:T(8,128)} %bitcast.58, f32[256,4096]{1,0:T(8,128)S(1)} %copy-done.3, f32[256]{0:T(256)S(1)} %fusion.13, f32[4096]{0:T(1024)S(1)} %bitcast.65), kind=kOutput, calls=%fused_computation.60 | convolution fusion | flops 3224633344 | bytes 14174208 | tf_op jit(solution)/shard_map/dot_general | solution.py:397
  88.8 0.1 copy.16
  88.9 0.1 mul.107
  89.1 6.1 %multiply_convert_fusion.1 = (bf16[2048,1024]{1,0:T(8,128)(2,1)S(1)}, f32[2048,1024]{1,0:T(8,128)}) fusion(f32[1024]{0:T(1024)S(1)} %copy-done.9, f32[2048]{0:T(1024)S(1)} %mul.113, bf16[512,1024]{1,0:T(8,128)(2,1)S(1)} %copy-done, f32[256,512]{1,0:T(8,128)S(1)} %get-tuple-element.18, f32[256,512]{1,0:T(8,128)S(1)} %get-tuple-element.4, f32[2048]{0:T(1024)S(1)} %mul.107), kind=kOutput, calls=%fused_computation.1 | convolution fusion | flops 2166358016 | bytes 14700544 | tf_op jit(solution)/shard_map/dot_general | solution.py:411
  95.2 3.7 %fusion.42 = (bf16[2048,512]{1,0:T(8,128)(2,1)}, f32[2048,512]{1,0:T(8,128)S(1)}) fusion(bf16[2048,1024]{1,0:T(8,128)(2,1)S(1)} %get-tuple-element.13, bf16[1024,512]{1,0:T(8,128)(2,1)S(1)} %copy-done.8), kind=kOutput, calls=%fused_computation.59 | convolution fusion | flops 2148532224 | bytes 11534336 | tf_op jit(solution)/shard_map/dot_general | solution.py:415
  98.9 2.5 %fusion.30 = f32[1024,512]{0,1:T(8,128)S(1)} fusion(bf16[2048,1024]{1,0:T(8,128)(2,1)S(1)} %get-tuple-element.13, f32[2048,512]{1,0:T(8,128)S(1)} %get-tuple-element.16, f32[256,512]{1,0:T(8,128)S(1)} %get-tuple-element.17), kind=kOutput, calls=%fused_computation.46 | convolution fusion | flops 2150629376 | bytes 11010048 | tf_op jit(solution)/shard_map/dot_general | solution.py:426
  101.4 0.2 fusion.41
  101.5 1.5 pad_maximum_fusion.1
  103.0 2.9 %copy.19 = f32[512,1024]{1,0:T(8,128)} copy(f32[512,1024]{0,1:T(8,128)} %pad_maximum_fusion.1) | data formatting | bytes 4194304 | tf_op jit(solution)/shard_map/concatenate | solution.py:428
  105.9 1.7 fusion.16
  107.6 4.0 %copy.18 = bf16[512,2048]{1,0:T(8,128)(2,1)} copy(bf16[512,2048]{0,1:T(8,128)(2,1)} %fusion.16) | data formatting | bytes 4194304 | tf_op jit(solution)/shard_map/dot_general | solution.py:425
  111.5 12.6 %fusion.26 = f32[1,4,4,4,8,1024]{5,4,3,2,1,0:T(8,128)} fusion(bf16[4,4,4,8,2048]{4,3,2,1,0:T(8,128)(2,1)} %bitcast.61, f32[2048,1024]{1,0:T(8,128)} %get-tuple-element.14, bf16[1024,512]{1,0:T(8,128)(2,1)} %param.11, f32[1024]{0:T(1024)S(1)} %copy-done.9, f32[2048]{0:T(1024)S(1)} %mul.113, f32[2048,512]{1,0:T(8,128)} %copy-done.10, f32[256,512]{1,0:T(8,128)S(1)} %copy-done.6), kind=kOutput, calls=%fused_computation.43 | convolution fusion | flops 4321181696 | bytes 18362368 | tf_op jit(solution)/shard_map/dot_general | solution.py:425
  124.2 4.0 %pad_maximum_fusion.in_ref = f32[2,4,4,4,8,1024]{5,4,3,2,1,0:T(8,128)} fusion(f32[1,4,4,4,8,1024]{5,4,3,2,1,0:T(8,128)S(1)} %bitcast.59, f32[1,4,4,4,8,1024]{5,4,3,2,1,0:T(8,128)} %fusion.26), kind=kLoop, calls=%fused_computation.8 | loop fusion | flops 1048576 | bytes 8388608 | tf_op jit(solution)/shard_map/stack | solution.py:431
  128.1 51.9 %sum_grads.1 = f32[2,4,4,4,8,1024]{5,4,3,2,1,0:T(8,128)} custom-call(f32[2,4,4,4,8,1024]{5,4,3,2,1,0:T(8,128)} %pad_maximum_fusion.in_ref), custom_call_target="tpu_custom_call" | custom-call | tf_op jit(solution)/shard_map/sum_grads/pallas_call | solution.py:341
  180.0 4.0 %fusion.39 = (f32[1,4,4,4,8,1024]{5,4,3,2,1,0:T(8,128)S(1)}, f32[1,4,4,4,8,1024]{5,4,3,2,1,0:T(8,128)}) fusion(f32[2,4,4,4,8,1024]{5,4,3,2,1,0:T(8,128)} %sum_grads.1), kind=kLoop, calls=%fused_computation.56 | loop fusion | bytes 8388608 | tf_op jit(solution)/shard_map/slice | solution.py:435
  184.0 0.2 fusion.40
  184.2 1.5 pad_maximum_fusion.2
  (24 shorter events, 0.2 us)
Async XLA Ops:
  0.6 88.4 %copy-start = (bf16[512,1024]{1,0:T(8,128)(2,1)S(1)}, bf16[512,1024]{1,0:T(8,128)(2,1)}, u32[]{:S(2)}) copy-start(bf16[512,1024]{1,0:T(8,128)(2,1)} %param.10) | copy-start | bytes 3145732
  55.8 2.0 %copy-start.2 = (f32[256,4096]{1,0:T(8,128)}, f32[256,4096]{1,0:T(8,128)S(1)}, u32[]{:S(2)}) copy-start(f32[256,4096]{1,0:T(8,128)S(1)} %get-tuple-element.12) | copy-start | bytes 12582916
  76.3 3.8 %copy-start.3 = (f32[256,4096]{1,0:T(8,128)S(1)}, f32[256,4096]{1,0:T(8,128)}, u32[]{:S(2)}) copy-start(f32[256,4096]{1,0:T(8,128)} %copy-done.2) | copy-start | bytes 12582916
  81.1 7.6 %copy-start.7 = (f32[256,8]{0,1:T(8,128)S(1)}, f32[256,8]{0,1:T(8,128)}, u32[]{:S(2)}) copy-start(f32[256,8]{0,1:T(8,128)} %param.8) | copy-start | bytes 24580
  81.1 7.9 %copy-start.9 = (f32[1024]{0:T(1024)S(1)}, f32[1024]{0:T(1024)}, u32[]{:S(2)}) copy-start(f32[1024]{0:T(1024)} %param.9) | copy-start | bytes 12292
  88.7 10.1 %copy-start.5 = (f32[256,512]{1,0:T(8,128)}, f32[256,512]{1,0:T(8,128)S(1)}, u32[]{:S(2)}) copy-start(f32[256,512]{1,0:T(8,128)S(1)} %get-tuple-element.17) | copy-start | bytes 1572868
  89.0 6.1 %copy-start.8 = (bf16[1024,512]{1,0:T(8,128)(2,1)S(1)}, bf16[1024,512]{1,0:T(8,128)(2,1)}, u32[]{:S(2)}) copy-start(bf16[1024,512]{1,0:T(8,128)(2,1)} %param.11) | copy-start | bytes 3145732
  98.8 2.5 %copy-start.10 = (f32[2048,512]{1,0:T(8,128)}, f32[2048,512]{1,0:T(8,128)S(1)}, u32[]{:S(2)}) copy-start(f32[2048,512]{1,0:T(8,128)S(1)} %get-tuple-element.16) | copy-start | bytes 12582916
  105.9 5.6 %copy-start.6 = (f32[256,512]{1,0:T(8,128)S(1)}, f32[256,512]{1,0:T(8,128)}, u32[]{:S(2)}) copy-start(f32[256,512]{1,0:T(8,128)} %copy-done.5) | copy-start | bytes 1572868
  111.5 12.6 %copy-start.4 = (f32[512,1024]{1,0:T(8,128)S(1)}, f32[512,1024]{1,0:T(8,128)}, u32[]{:S(2)}) copy-start(f32[512,1024]{1,0:T(8,128)} %copy.19) | copy-start | bytes 6291460
  184.0 1.7 copy-start.1

commit v2 on v1

--- a/solution.py
+++ b/solution.py
@@ -9,7 +9,6 @@
 from jax.sharding import PartitionSpec as P
 
 ENTROPY = 0.05
-HIGH_PREC = lax.Precision.HIGH
 MESH = pl.DeviceIdType.MESH
 VMEM_CAP = 60 * 1024 * 1024
 
@@ -29,8 +28,9 @@
         self.q = tuple(u * 2 + v for u, v in self.groups)
         self.row, self.col = row, col
 
-    def partner(self, group, flip):
+    def partner(self, group, flip, cross=0):
         hi, lo = flip // 2, flip % 2
+        core = 1 - self.core if cross else self.core
         groups = [list(g) for g in self.groups]
         if hi:
             groups[group][0] = 1 - groups[group][0]
@@ -38,7 +38,7 @@
             groups[group][1] = 1 - groups[group][1]
         (xa, ya), (yb, za), (zb, xb) = groups
         x, y, z = ((2 * b + (a + b) % 2) for a, b in ((xa, xb), (ya, yb), (za, zb)))
-        return (y * 2 + x // 2, z * 4 + (x % 2) * 2 + self.core)
+        return (y * 2 + x // 2, z * 4 + (x % 2) * 2 + core)
 
     def other_core(self):
         return (self.row, self.col + 1 - 2 * self.core)
@@ -122,22 +122,201 @@
         made.wait_send()
 
 
-def data_kernel(pieces, data_ref, out_ref, local_sem, send_sem, recv_sem):
+def meet_all(place):
+    barrier = pltpu.get_barrier_semaphore()
+    known = [place.other_core()]
+    for group, both in ((0, True), (1, False), (2, True)):
+        for flip in (1, 2, 3):
+            known.append(place.partner(group, flip))
+            if both:
+                known.append(place.partner(group, flip, 1))
+    for device in known:
+        pl.semaphore_signal(barrier, inc=1, device_id=device, device_id_type=MESH)
+    pl.semaphore_wait(barrier, len(known))
+
+
+def joined(pairs):
+    peak = pairs[0][0]
+    for other, _ in pairs[1:]:
+        peak = jnp.maximum(peak, other)
+    total = pairs[0][1] * jnp.exp(pairs[0][0] - peak)
+    for other, amount in pairs[1:]:
+        total = total + amount * jnp.exp(other - peak)
+    return peak, total
+
+
+def join_columns(place, pairs, held, slots, send, recv, base):
+    core = place.core
+    started = []
+
+    def copy(src, dst, number, device):
+        made = pltpu.make_async_remote_copy(
+            src_ref=src, dst_ref=dst, send_sem=send.at[number], recv_sem=recv.at[number],
+            device_id=device, device_id_type=MESH,
+        )
+        made.start()
+        started.append(made)
+        return made
+
+    def device(group, flip, cross):
+        return place.other_core() if flip == 0 else place.partner(group, flip, cross)
+
+    ways = [(flip, cross) for flip in range(4) for cross in range(2) if flip or cross]
+    now = []
+    for flip, cross in ways:
+        k = 2 * flip + cross
+        half = 1 - core if cross else core
+        now.append(copy(pairs.at[half], slots.at[0, k], base + k, device(0, flip, cross)))
+    for made in now:
+        made.wait_recv()
+    found = [(pairs[core, 0], pairs[core, 1])]
+    found += [(slots[0, 2 * f + c, 0], slots[0, 2 * f + c, 1]) for f, c in ways]
+    held[0, 0], held[0, 1] = joined(found)
+    now = []
+    for flip in (1, 2, 3):
+        number = base + 8 + flip
+        now.append(copy(held.at[0], slots.at[1, flip], number, device(1, flip, 0)))
+    for made in now:
+        made.wait_recv()
+    found = [(held[0, 0], held[0, 1])]
+    found += [(slots[1, flip, 0], slots[1, flip, 1]) for flip in (1, 2, 3)]
+    held[1, 0], held[1, 1] = joined(found)
+    now = []
+    for flip, cross in ways:
+        k = 2 * flip + cross
+        now.append(copy(held.at[1], slots.at[2, k], base + 16 + k, device(2, flip, cross)))
+    for made in now:
+        made.wait_recv()
+    found = [(held[1, 0], held[1, 1])]
+    found += [(slots[2, 2 * flip, 0], slots[2, 2 * flip, 1]) for flip in (1, 2, 3)]
+    own = joined(found)
+    other = joined([(slots[2, 2 * flip + 1, 0], slots[2, 2 * flip + 1, 1]) for flip in range(4)])
+    return own, other, started
+
+
+def target_kernel(
+    pieces, total_noise, data_ref, noise_ref, target_ref, data, data_hi, data_lo, anchor, anchor_hi,
+    anchor_lo, score, running, pairs, held, slots, local_sem, send_sem, recv_sem,
+):
     place = Place()
-    rows = out_ref.shape[4]
+    f32, bf16 = jnp.float32, jnp.bfloat16
+    rows = data.shape[4]
+    share, width = anchor.shape
+    chunks, _, chunk = score.shape
+    total_data = chunks * chunk
     start = pl.multiple_of(place.row * rows, rows)
-    unit = out_ref.at[(place.core, *place.q)]
-    bring = pltpu.make_async_copy(data_ref.at[pl.ds(start, rows)], unit, local_sem)
+    unit = data.at[(place.core, *place.q)]
+    bring = pltpu.make_async_copy(data_ref.at[pl.ds(start, rows)], unit, local_sem.at[0])
     bring.start()
-    meet(place)
+    first = pl.multiple_of(place.col * share, share)
+    noise = pltpu.make_async_copy(noise_ref.at[pl.ds(first, share)], anchor, local_sem.at[1])
+    noise.start()
+    meet_all(place)
     bring.wait()
-    gather_phases(place, out_ref, pieces, (send_sem, recv_sem), 0)
-
-
-def gather_data(data_points):
+    noise.wait()
+    x = anchor[...]
+    high = x.astype(bf16)
+    anchor_hi[...] = high
+    anchor_lo[...] = (x - high.astype(f32)).astype(bf16)
+    noise_sq = jnp.sum(x * x, axis=1, keepdims=True)
+    gather_phases(place, data, pieces, (send_sem, recv_sem), 0)
+
+    across = (((1,), (1,)), ((), ()))
+    lanes = 128
+    tiles = chunk // lanes
+    running[...] = jnp.full_like(running, -jnp.inf)
+
+    @pl.loop(0, chunks)
+    def _(i):
+        points = data[i // 8, (i // 2) % 4, pl.ds((i % 2) * 2, 2)].reshape(chunk, width)
+        high = points.astype(bf16)
+        low = (points - high.astype(f32)).astype(bf16)
+        data_hi[i] = high
+        data_lo[i] = low
+        square = points * points
+        part = square[:, :lanes]
+        for k in range(1, width // lanes):
+            part = part + square[:, k * lanes : (k + 1) * lanes]
+        data_sq = jnp.sum(part.T, axis=0, keepdims=True)
+        inner = lax.dot_general(anchor_hi[...], high, across, preferred_element_type=f32)
+        inner += lax.dot_general(anchor_hi[...], low, across, preferred_element_type=f32)
+        inner += lax.dot_general(anchor_lo[...], high, across, preferred_element_type=f32)
+        cost = (noise_sq + data_sq - 2.0 * inner) * (1.0 / width)
+        found = cost * (-1.0 / ENTROPY)
+        score[i] = found
+        peak = running[...]
+        for k in range(tiles):
+            peak = jnp.maximum(peak, found[:, k * lanes : (k + 1) * lanes])
+        running[...] = peak
+
+    peak = jnp.max(running[...], axis=1, keepdims=True)
+    running[...] = jnp.zeros_like(running)
+
+    @pl.loop(0, chunks)
+    def _(i):
+        e = jnp.exp(score[i] - peak)
+        total = running[...]
+        for k in range(tiles):
+            total = total + e[:, k * lanes : (k + 1) * lanes]
+        running[...] = total
+
+    total = jnp.sum(running[...], axis=1, keepdims=True)
+    row_lse = peak + jnp.log(total) - math.log(float(total_data))
+
+    @pl.loop(0, chunks)
+    def _(i):
+        s = score[i] - row_lse
+        col_peak = jnp.max(s, axis=0, keepdims=True)
+        col_total = jnp.sum(jnp.exp(s - col_peak), axis=0, keepdims=True)
+        for k in range(tiles):
+            at = i * tiles + k
+            cols = slice(k * lanes, (k + 1) * lanes)
+            pairs[at // 16, 0, pl.ds(at % 16, 1), :] = col_peak[:, cols]
+            pairs[at // 16, 1, pl.ds(at % 16, 1), :] = col_total[:, cols]
+
+    base = 13 * len(pieces)
+    own, other, started = join_columns(place, pairs, held, slots, send_sem, recv_sem, base)
+    for made in started:
+        made.wait_send()
+    log_noise = math.log(float(total_noise))
+    pairs[place.core, 0] = own[0] + jnp.log(own[1]) - log_noise
+    pairs[1 - place.core, 0] = other[0] + jnp.log(other[1]) - log_noise
+    running[...] = jnp.full_like(running, -jnp.inf)
+
+    @pl.loop(0, chunks)
+    def _(i):
+        peak = running[...]
+        for k in range(tiles):
+            at = i * tiles + k
+            cols = slice(k * lanes, (k + 1) * lanes)
+            s = score[i, :, cols] - pairs[at // 16, 0, pl.ds(at % 16, 1), :]
+            score[i, :, cols] = s
+            peak = jnp.maximum(peak, s)
+        running[...] = peak
+
+    peak = jnp.max(running[...], axis=1, keepdims=True)
+    running[...] = jnp.zeros_like(running)
+    target_ref[...] = jnp.zeros_like(target_ref)
+
+    @pl.loop(0, chunks)
+    def _(i):
+        weights = jnp.exp(score[i] - peak).astype(bf16)
+        total = running[...]
+        for k in range(tiles):
+            total = total + weights[:, k * lanes : (k + 1) * lanes].astype(f32)
+        running[...] = total
+        target_ref[...] += jnp.dot(
+            weights, data_hi[i], preferred_element_type=f32
+        ) + jnp.dot(weights, data_lo[i], preferred_element_type=f32)
+
+    target_ref[...] = target_ref[...] / jnp.sum(running[...], axis=1, keepdims=True)
+
+
+def find_target(noise_points, data_points, total_noise, share):
     count, width = data_points.shape
     peers = lax.axis_size("row")
     rows = count // peers
+    total_data = count * lax.axis_size("col")
     quarter, tile = rows // 4, width // 4
     every = slice(None)
     last = slice(3 * quarter, rows)
@@ -149,94 +328,37 @@
         (last, slice(tile, 2 * tile), 1),
         (last, slice(2 * tile, width), 2),
     )
-    copies = 13 * len(pieces)
-    out = pl.pallas_call(
-        functools.partial(data_kernel, pieces),
-        out_shape=jax.ShapeDtypeStruct((2, 4, 4, 4, rows, width), data_points.dtype),
-        in_specs=[pl.BlockSpec(memory_space=pl.ANY)],
+    copies = 13 * len(pieces) + 24
+    chunk = 8 * rows
+    chunks = total_data // chunk
+    f32, bf16 = jnp.float32, jnp.bfloat16
+    half = (2, total_data // 256, 128)
+    return pl.pallas_call(
+        functools.partial(target_kernel, pieces, total_noise),
+        out_shape=jax.ShapeDtypeStruct((share, width), f32),
+        in_specs=[pl.BlockSpec(memory_space=pl.ANY)] * 2,
         out_specs=pl.BlockSpec(memory_space=pltpu.VMEM),
         scratch_shapes=[
-            pltpu.SemaphoreType.DMA,
+            pltpu.VMEM((2, 4, 4, 4, rows, width), f32),
+            pltpu.VMEM((chunks, chunk, width), bf16),
+            pltpu.VMEM((chunks, chunk, width), bf16),
+            pltpu.VMEM((share, width), f32),
+            pltpu.VMEM((share, width), bf16),
+            pltpu.VMEM((share, width), bf16),
+            pltpu.VMEM((chunks, share, chunk), f32),
+            pltpu.VMEM((share, 128), f32),
+            pltpu.VMEM((2, *half), f32),
+            pltpu.VMEM((2, *half), f32),
+            pltpu.VMEM((3, 8, *half), f32),
+            pltpu.SemaphoreType.DMA((2,)),
             pltpu.SemaphoreType.DMA((copies,)),
             pltpu.SemaphoreType.DMA((copies,)),
         ],
         compiler_params=pltpu.CompilerParams(
             collective_id=1, has_side_effects=True, vmem_limit_bytes=VMEM_CAP
         ),
-        name="gather_data",
-    )(data_points)
-    return out.reshape(-1, width)
-
-
-def join_pairs(first, second):
-    peak = jnp.maximum(first[0], second[0])
-    total = first[1] * jnp.exp(first[0] - peak) + second[1] * jnp.exp(second[0] - peak)
-    return peak, total
-
-
-def columns_kernel(in_ref, out_ref, held, slots, from_core, send_sem, recv_sem):
-    place = Place()
-    core = place.core
-    meet(place)
-
-    def copy(src, dst, number, device):
-        made = pltpu.make_async_remote_copy(
-            src_ref=src, dst_ref=dst, send_sem=send_sem.at[number], recv_sem=recv_sem.at[number],
-            device_id=device, device_id_type=MESH,
-        )
-        made.start()
-        return made
-
-    other = 1 - core
-    started = [copy(in_ref.at[other], from_core, 0, place.other_core())]
-    started[0].wait_recv()
-    own = in_ref[core]
-    got = from_core[...]
-    pair = join_pairs((own[0], own[1]), (got[0], got[1]))
-    for group in range(3):
-        held[group, 0] = pair[0]
-        held[group, 1] = pair[1]
-        now = [
-            copy(held.at[group], slots.at[group, flip - 1], 3 * group + flip,
-                 place.partner(group, flip))
-            for flip in (1, 2, 3)
-        ]
-        started += now
-        for flip in (1, 2, 3):
-            now[flip - 1].wait_recv()
-        new_peak = pair[0]
-        for k in range(3):
-            new_peak = jnp.maximum(new_peak, slots[group, k, 0])
-        total = pair[1] * jnp.exp(pair[0] - new_peak)
-        for k in range(3):
-            total = total + slots[group, k, 1] * jnp.exp(slots[group, k, 0] - new_peak)
-        pair = (new_peak, total)
-    out_ref[core, 0] = pair[0]
-    out_ref[core, 1] = pair[1]
-    final = copy(out_ref.at[core], out_ref.at[core], 10, place.other_core())
-    started.append(final)
-    final.wait_recv()
-    for made in started:
-        made.wait_send()
-
-
-def join_columns(pairs):
-    shape = pairs.shape
-    return pl.pallas_call(
-        columns_kernel,
-        out_shape=jax.ShapeDtypeStruct(shape, pairs.dtype),
-        in_specs=[pl.BlockSpec(memory_space=pltpu.VMEM)],
-        out_specs=pl.BlockSpec(memory_space=pltpu.VMEM),
-        scratch_shapes=[
-            pltpu.VMEM((3, *shape[1:]), jnp.float32),
-            pltpu.VMEM((3, 3, *shape[1:]), jnp.float32),
-            pltpu.VMEM(shape[1:], jnp.float32),
-            pltpu.SemaphoreType.DMA((11,)),
-            pltpu.SemaphoreType.DMA((11,)),
-        ],
-        compiler_params=pltpu.CompilerParams(collective_id=2, has_side_effects=True),
-        name="join_columns",
-    )(pairs)
+        name="find_target",
+    )(data_points, noise_points)
 
 
 def grads_kernel(pieces, in_ref, out_ref, acc, from_core, slot_0, slot_1, slot_2, send_sem, recv_sem):
@@ -359,76 +481,119 @@
     )(grads)
 
 
+def spread(rows, steps_each):
+    count, width = rows.shape
+    wide = jnp.broadcast_to(rows[:, None, :], (count, steps_each, width))
+    return wide.reshape(count * steps_each, width)
+
+
+def train_kernel(
+    scale, points, steps_each, anchor_ref, target_ref, tvals_ref, shift_ref, w_in_ref, w_out_ref,
+    w_back_ref, predicted_ref, grads_ref, mixed_ref, hidden_ref, delta_ref, delta_pre_ref,
+):
+    block = points * steps_each
+    width, hid_width = w_in_ref.shape
+    blocks = anchor_ref.shape[0] // points
+    grads_ref[...] = jnp.zeros_like(grads_ref)
+    f32, bf16 = jnp.float32, jnp.bfloat16
+    contract = (((0,), (0,)), ((), ()))
+    lanes = 128
+
+    def forward(b, slot):
+        here = pl.ds(pl.multiple_of(b * points, points), points)
+        anchor, target = anchor_ref[here, :], target_ref[here, :]
+        tvals = tvals_ref[pl.ds(pl.multiple_of(b * block, block), block), :]
+        parts = []
+        for k in range(width // lanes):
+            cols = slice(k * lanes, (k + 1) * lanes)
+            x, y = spread(anchor[:, cols], steps_each), spread(target[:, cols], steps_each)
+            parts.append(((1.0 - tvals) * x + tvals * y).astype(bf16))
+        mixed = jnp.concatenate(parts, axis=1)
+        mixed_ref[slot] = mixed
+        pre = jnp.dot(mixed, w_in_ref[...], preferred_element_type=f32)
+        shift = jnp.concatenate(
+            [tvals * shift_ref[:, k * lanes : (k + 1) * lanes] for k in range(hid_width // lanes)],
+            axis=1,
+        )
+        pre = pre + shift
+        sig = 0.5 * jnp.tanh(0.5 * pre) + 0.5
+        hidden = (pre * sig).astype(bf16)
+        slope = sig * (1.0 + pre * (1.0 - sig))
+        hidden_ref[slot] = hidden
+        output = jnp.dot(hidden, w_out_ref[...], preferred_element_type=f32)
+        predicted_ref[pl.ds(pl.multiple_of(b * block, block), block), :] = output.astype(bf16)
+        velocity = spread(target - anchor, steps_each)
+        delta = ((output - velocity) * scale).astype(bf16)
+        delta_ref[slot] = delta
+        back = jnp.dot(delta, w_back_ref[...], preferred_element_type=f32)
+        delta_pre_ref[slot] = (back * slope).astype(bf16)
+
+    def add_grads(slot):
+        grads_ref[0] += lax.dot_general(
+            mixed_ref[slot], delta_pre_ref[slot], contract, preferred_element_type=f32
+        )
+        for k in range(hid_width // width):
+            cols = slice(k * width, (k + 1) * width)
+            grads_ref[1, :, cols] += lax.dot_general(
+                hidden_ref[slot, :, cols], delta_ref[slot], contract, preferred_element_type=f32
+            )
+
+    forward(0, 0)
+
+    @pl.loop(1, blocks)
+    def _(b):
+        forward(b, b % 2)
+        add_grads((b + 1) % 2)
+
+    add_grads((blocks - 1) % 2)
+
+
+def train(anchor, target, times, time_shift, weight_in, weight_out, scale):
+    share, width = anchor.shape
+    hid_width = weight_in.shape[1]
+    steps_each = times.shape[1]
+    points = 32
+    block = points * steps_each
+    tvals = jnp.broadcast_to(times.reshape(share * steps_each, 1), (share * steps_each, 128))
+    bf16 = jnp.bfloat16
+    vmem = pl.BlockSpec(memory_space=pltpu.VMEM)
+    return pl.pallas_call(
+        functools.partial(train_kernel, scale, points, steps_each),
+        out_shape=(
+            jax.ShapeDtypeStruct((share * steps_each, width), bf16),
+            jax.ShapeDtypeStruct((2, width, hid_width), jnp.float32),
+        ),
+        in_specs=[vmem] * 7,
+        out_specs=(vmem, vmem),
+        scratch_shapes=[
+            pltpu.VMEM((2, block, width), bf16),
+            pltpu.VMEM((2, block, hid_width), bf16),
+            pltpu.VMEM((2, block, width), bf16),
+            pltpu.VMEM((2, block, hid_width), bf16),
+        ],
+        compiler_params=pltpu.CompilerParams(vmem_limit_bytes=VMEM_CAP),
+        name="train",
+    )(anchor, target, tvals, time_shift.reshape(1, hid_width), weight_in, weight_out, weight_out.T)
+
+
 def on_device(noise_points, data_points, times, time_shift, weight_in, weight_out):
     count_row = lax.axis_size("row")
     count_col = lax.axis_size("col")
     rows_here = noise_points.shape[0]
     total_noise = rows_here * count_row
-    total_data = data_points.shape[0] * count_col
     width = noise_points.shape[1]
     share = rows_here // count_col
     steps_each = times.shape[1]
 
-    data_all = gather_data(data_points)
+    target = find_target(noise_points, data_points, total_noise, share)
     anchor = lax.dynamic_slice_in_dim(noise_points, lax.axis_index("col") * share, share, 0)
-    noise_sq = jnp.sum(anchor * anchor, axis=1)
-    data_sq = jnp.sum(data_all * data_all, axis=1)
-    inner = lax.dot_general(
-        anchor, data_all, (((1,), (1,)), ((), ())), precision=HIGH_PREC,
-        preferred_element_type=jnp.float32,
-    )
-    cost = (noise_sq[:, None] + data_sq[None, :] - 2.0 * inner) / width
-    scores = -cost / ENTROPY
-    row_peak = jnp.max(scores, axis=1)
-    row_total = jnp.sum(jnp.exp(scores - row_peak[:, None]), axis=1)
-    potential_f = -ENTROPY * (row_peak + jnp.log(row_total) - math.log(float(total_data)))
-    scores = (potential_f[:, None] - cost) / ENTROPY
-    local_peak = jnp.max(scores, axis=0)
-    local_total = jnp.sum(jnp.exp(scores - local_peak[None, :]), axis=0)
-    pairs = jnp.stack(
-        [local_peak.reshape(2, -1, 128), local_total.reshape(2, -1, 128)], axis=1
-    )
-    joined = join_columns(pairs)
-    col_peak, col_total = joined[:, 0].reshape(-1), joined[:, 1].reshape(-1)
-    potential_g = -ENTROPY * (col_peak + jnp.log(col_total) - math.log(float(total_noise)))
-    scores = (potential_g[None, :] - cost) / ENTROPY
-    final_peak = jnp.max(scores, axis=1)
-    weights = jnp.exp(scores - final_peak[:, None])
-    numer = jnp.dot(weights, data_all, precision=HIGH_PREC, preferred_element_type=jnp.float32)
-    target = numer / jnp.sum(weights, axis=1)[:, None]
-
-    tvals = times[:, :, None]
-    mixed = (
-        ((1.0 - tvals) * anchor[:, None, :] + tvals * target[:, None, :])
-        .reshape(share * steps_each, width)
-        .astype(jnp.bfloat16)
-    )
-    velocity = jnp.broadcast_to((target - anchor)[:, None, :], (share, steps_each, width)).reshape(
-        share * steps_each, width
+    scale = 1.0 / math.sqrt(float(total_noise * steps_each))
+    predicted, grads = train(
+        anchor, target, times, time_shift, weight_in, weight_out, scale
     )
     hid_width = weight_in.shape[1]
-    pre = (
-        jnp.dot(mixed, weight_in, preferred_element_type=jnp.float32)
-        + times.reshape(share * steps_each, 1) * time_shift[None, :]
-    )
-    hidden = jax.nn.silu(pre).astype(jnp.bfloat16)
-    output = jnp.dot(hidden, weight_out, preferred_element_type=jnp.float32)
-    predicted = output.astype(jnp.bfloat16)
-    scale = 1.0 / math.sqrt(float(total_noise * steps_each))
-    delta = ((output - velocity) * scale).astype(jnp.bfloat16)
-    back = lax.dot_general(
-        delta, weight_out, (((1,), (1,)), ((), ())), preferred_element_type=jnp.float32
-    )
-    sig = jax.nn.sigmoid(pre)
-    delta_pre = (back * sig * (1.0 + pre * (1.0 - sig))).astype(jnp.bfloat16)
-    contract = (((0,), (0,)), ((), ()))
-    first = lax.dot_general(mixed, delta_pre, contract, preferred_element_type=jnp.float32)
-    second = lax.dot_general(hidden, delta, contract, preferred_element_type=jnp.float32)
     halves = hid_width // width
-    second = jnp.concatenate(
-        [second[k * width : (k + 1) * width] for k in range(halves)], axis=1
-    )
-    grads = jnp.stack([first, second]).reshape(2, 4, 4, 4, width // 64, hid_width)
+    grads = grads.reshape(2, 4, 4, 4, width // 64, hid_width)
     summed = sum_grads(grads).reshape(2, width, hid_width)
     grad_in = summed[0]
     grad_out = jnp.concatenate(

time: 186 us -> 152 us (0.82)
  matrix products: 39 us -> 0 us
  Pallas kernels: 111 us -> 140 us
  other arithmetic: 21.6 us -> 1.49 us
  local copies, waits for them, and re-layouts: 13.1 us -> 9.6 us
    dot_general x6 -> x0, matrix products: 39 us -> none  [the longest x1 12.6 us: on_device(): lax.dot_general(mixed, delta_pre, contract, preferred_element_type=jnp.fl...]
    pallas_call x2, Pallas kernels: 59.3 us -> 88.1 us  [the longest x1 67.4 us: find_target(): pl.pallas_call(functools.partial(target_kernel, pieces, total_noise), out...]
    reduce_sum x5 -> x0, other arithmetic: 7.91 us -> none  [the longest x1 4.07 us: on_device(): data_sq = jnp.sum(data_all * data_all, axis=1)]
    another operation x2 -> x0, other arithmetic: 4.57 us -> none  [the longest x1 3.96 us: on_device(): jnp.stack([first, second]).reshape(2, 4, 4, 4, width // 64, hid_width)]
    dot_general x1 -> x0, local copies, waits for them, and re-layouts: 3.96 us -> none  [on_device(): lax.dot_general(mixed, delta_pre, contract, preferred_element_type=jnp.fl...]
    reduce_max x2 -> x0, other arithmetic: 3.55 us -> none  [the longest x1 2.93 us: on_device(): final_peak = jnp.max(scores, axis=1)]
    concatenate x1 -> x0, local copies, waits for them, and re-layouts: 2.88 us -> none  [on_device(): jnp.concatenate([second[k * width:(k + 1) * width] for k in range(halves)...]
    dynamic_slice x0 -> x1, local copies, waits for them, and re-layouts: none -> 1.89 us  [on_device(): lax.dynamic_slice_in_dim(noise_points, lax.axis_index('col') * share, sha...]
where the time goes in v2:
time: 152 us; the launch traced here: 151 us
  Pallas kernels  140 us (92%)
  local copies, waits for them, and re-layouts  9.6 us (6%)
    pallas_call x1, Pallas kernels, find_target(): pl.pallas_call(functools.partial(target_kernel, pieces, total_noise), out...  67.4 us
    pallas_call x1, Pallas kernels, sum_grads(): pl.pallas_call(functools.partial(grads_kernel, pieces), out_shape=jax.Sha...  51.6 us
    pallas_call x1, Pallas kernels, train(): pl.pallas_call(functools.partial(train_kernel, scale, points, steps_each)...  20.7 us
    slice x2, local copies, waits for them, and re-layouts, on_device(): summed[1][:, k * width:(k + 1) * width]  4.17 us

profile of v2, /device:TPU:1, one launch (start us, length us, event | category | flops | bytes accessed | tf_op | source)
XLA Modules:
  0.0 151.4 jit_solution(14673021662694409700)
XLA Ops:
  0.6 0.8 copy.10
  1.5 0.1 broadcast_in_dim.7
  1.6 1.9 %constant_dynamic-slice_fusion.anchor_ref = f32[256,512]{1,0:T(8,128)} fusion(f32[4096,512]{1,0:T(8,128)} %noise_ref.1, s32[]{:T(128)S(6)} %select_n.3), kind=kLoop, calls=%fused_computation.1 | loop fusion | bytes 1048580 | tf_op jit(solution)/shard_map/dynamic_slice | solution.py:589
  3.5 0.0 copy-start
  3.5 67.4 %find_target.1.target_ref = f32[256,512]{1,0:T(8,128)} custom-call(f32[256,512]{1,0:T(8,128)} %data_ref.1, f32[4096,512]{1,0:T(8,128)} %noise_ref.1), custom_call_target="tpu_custom_call" | custom-call | tf_op jit(solution)/shard_map/find_target/pallas_call | solution.py:336
  70.9 1.3 broadcast_in_dim.8.tvals_ref
  72.2 0.0 copy-done
  72.2 1.3 copy.11
  73.5 20.7 %train.1 = (bf16[2048,512]{1,0:T(8,128)(2,1)}, f32[2,512,1024]{2,1,0:T(8,128)}) custom-call(f32[256,512]{1,0:T(8,128)} %constant_dynamic-slice_fusion.anchor_ref, f32[256,512]{1,0:T(8,128)} %find_target.1.target_ref, f32[2048,128]{1,0:T(8,128)} %broadcast_in_dim.8.tvals_ref, f32[1,1024]{1,0:T(1,128)} %bitcast.9, bf16[512,1024]{1,0:T(8,128)(2,1)} %w_in_ref.1, ...), custom_call_target="tpu_custom_call" | custom-call | tf_op jit(solution)/shard_map/train/pallas_call | solution.py:560
  94.2 51.6 %sum_grads.1 = f32[2,4,4,4,8,1024]{5,4,3,2,1,0:T(8,128)} custom-call(f32[2,4,4,4,8,1024]{5,4,3,2,1,0:T(8,128)} %bitcast.6), custom_call_target="tpu_custom_call" | custom-call | tf_op jit(solution)/shard_map/sum_grads/pallas_call | solution.py:463
  145.8 4.0 %fusion = (f32[1,4,4,4,8,1024]{5,4,3,2,1,0:T(8,128)S(1)}, f32[1,4,4,4,8,1024]{5,4,3,2,1,0:T(8,128)}) fusion(f32[2,4,4,4,8,1024]{5,4,3,2,1,0:T(8,128)} %sum_grads.1), kind=kLoop, calls=%fused_computation.2 | loop fusion | bytes 8388608 | tf_op jit(solution)/shard_map/slice | solution.py:600
  149.8 0.2 fusion.1
  150.0 1.5 pad_maximum_fusion
Async XLA Ops:
  3.5 68.7 %copy-start = (bf16[1024,512]{1,0:T(8,128)(2,1)S(1)}, bf16[1024,512]{1,0:T(8,128)(2,1)}, u32[]{:S(2)}) copy-start(bf16[1024,512]{1,0:T(8,128)(2,1)} %w_out_ref.1) | copy-start | bytes 3145732

commit v3 on v2

--- a/solution.py
+++ b/solution.py
@@ -11,6 +11,7 @@
 ENTROPY = 0.05
 MESH = pl.DeviceIdType.MESH
 VMEM_CAP = 60 * 1024 * 1024
+GATHERS = 19
 
 
 class Place:
@@ -71,14 +72,14 @@
     return tuple(found)
 
 
-def gather_phases(place, out, pieces, sems, base):
+def gather_phases(place, out, pieces, sems, base, phases=(0, 1, 2)):
     send, recv = sems
     mine = out.at[place.core]
     started = []
 
-    def copy(src, dst, number, device):
+    def copy(block, number, device):
         made = pltpu.make_async_remote_copy(
-            src_ref=src, dst_ref=dst, send_sem=send.at[number], recv_sem=recv.at[number],
+            src_ref=block, dst_ref=block, send_sem=send.at[number], recv_sem=recv.at[number],
             device_id=device, device_id_type=MESH,
         )
         made.start()
@@ -90,32 +91,52 @@
         return mine.at[(*at_groups(turn, *values), rows, cols)]
 
     waiting = [[] for _ in pieces]
-    for phase in range(3):
+    for phase in phases[:-1]:
         for n, piece in enumerate(pieces):
             turn = piece[2]
             q = [place.q[(turn + k) % 3] for k in range(3)]
             for made in waiting[n]:
                 made.wait_recv()
             waiting[n] = []
-            held = (q, q[:2], q[:1])[phase]
             group = (turn + 2 - phase) % 3
-            block = spot(piece, *held)
+            block = spot(piece, *(q, q[:2])[phase])
             for flip in (1, 2, 3):
-                number = base + (n * 3 + phase) * 3 + flip - 1
-                waiting[n].append(copy(block, block, number, place.partner(group, flip)))
-    first = base + 9 * len(pieces)
-    across = []
+                number = base + GATHERS * n + phase * 3 + flip - 1
+                waiting[n].append(copy(block, number, place.partner(group, flip)))
+    halves = (pl.ds(0, 2), pl.ds(2, 2))
+    across, landed = [], []
     for n, piece in enumerate(pieces):
         turn = piece[2]
+        for made in waiting[n]:
+            made.wait_recv()
+        first = base + GATHERS * n + 6
         own = place.q[turn]
-        block = spot(piece, own)
-        across.append(copy(block, block, first + 4 * n, place.other_core()))
-    for n, piece in enumerate(pieces):
-        turn = piece[2]
-        for flip in (1, 2, 3):
-            waiting[n][flip - 1].wait_recv()
-            block = spot(piece, place.flipped(turn, flip))
-            across.append(copy(block, block, first + 4 * n + flip, place.other_core()))
+        now = {}
+        for k in range(2):
+            for flip, half in ((2, k), (1, 1 - k)):
+                block = spot(piece, own, halves[half])
+                now[flip, half] = copy(block, first + 2 * (flip - 1) + half,
+                                       place.partner(turn, flip))
+        across.append(copy(spot(piece, own), first + 6, place.other_core()))
+        landed.append(now)
+    for flip, half, step in ((2, 0, 0), (1, 1, 0), (2, 1, 1), (1, 0, 1)):
+        for n, piece in enumerate(pieces):
+            turn = piece[2]
+            first = base + GATHERS * n + 6
+            landed[n][flip, half].wait_recv()
+            block = spot(piece, place.flipped(turn, flip), halves[half])
+            if step == 0:
+                landed[n][3, half] = copy(block, first + 4 + half, place.partner(turn, 3 - flip))
+            across.append(
+                copy(block, first + 7 + 2 * (flip - 1) + half, place.other_core())
+            )
+    for half in range(2):
+        for n, piece in enumerate(pieces):
+            turn = piece[2]
+            first = base + GATHERS * n + 6
+            landed[n][3, half].wait_recv()
+            block = spot(piece, place.flipped(turn, 3), halves[half])
+            across.append(copy(block, first + 11 + half, place.other_core()))
     for made in across:
         made.wait_recv()
     for made in started:
@@ -274,7 +295,7 @@
             pairs[at // 16, 0, pl.ds(at % 16, 1), :] = col_peak[:, cols]
             pairs[at // 16, 1, pl.ds(at % 16, 1), :] = col_total[:, cols]
 
-    base = 13 * len(pieces)
+    base = GATHERS * len(pieces)
     own, other, started = join_columns(place, pairs, held, slots, send_sem, recv_sem, base)
     for made in started:
         made.wait_send()
@@ -328,7 +349,7 @@
         (last, slice(tile, 2 * tile), 1),
         (last, slice(2 * tile, width), 2),
     )
-    copies = 13 * len(pieces) + 24
+    copies = GATHERS * len(pieces) + 24
     chunk = 8 * rows
     chunks = total_data // chunk
     f32, bf16 = jnp.float32, jnp.bfloat16
@@ -361,7 +382,9 @@
     )(data_points, noise_points)
 
 
-def grads_kernel(pieces, in_ref, out_ref, acc, from_core, slot_0, slot_1, slot_2, send_sem, recv_sem):
+def grads_kernel(
+    pieces, in_ref, out_ref, acc, from_core, slot_0, slot_1, slot_2, send_sem, recv_sem
+):
     place = Place()
     core = place.core
     meet(place)
@@ -373,79 +396,111 @@
             device_id=device, device_id_type=MESH,
         )
         made.start()
+        started.append(made)
         return made
 
     every = slice(None)
     other = 1 - core
     started = []
     first = []
-    for n, (rows, cols, turn) in enumerate(pieces):
-        made = copy(in_ref.at[other, :, :, :, :, cols], from_core.at[:, :, :, :, cols], n,
-                    place.other_core())
-        first.append(made)
-    started += first
+    for n, (_, cols, turn) in enumerate(pieces):
+        first.append(copy(in_ref.at[other, :, :, :, :, cols], from_core.at[:, :, :, :, cols], n,
+                          place.other_core()))
     base = count
-    waiting = [[] for _ in pieces]
-    for n, (rows, cols, turn) in enumerate(pieces):
+    halves = (pl.ds(0, 2), pl.ds(2, 2))
+    landed = []
+
+    def part(turn, flip, half, cols):
+        lead = at_groups(turn, place.flipped(turn, flip), halves[half])
+        return (*lead, every, cols)
+
+    for n, (_, cols, turn) in enumerate(pieces):
         first[n].wait_recv()
+        wide = slice(0, cols.stop - cols.start)
 
         @pl.loop(0, 16)
         def _(i, cols=cols):
             a, b = i // 4, i % 4
             acc[a, b, :, :, cols] = in_ref[core, a, b, :, :, cols] + from_core[a, b, :, :, cols]
 
+        now = {}
+        for flip, half, kind in ((3, 0, 0), (3, 1, 0), (1, 0, 1), (2, 1, 1)):
+            way = 1 + half if kind == 0 else flip
+            number = base + n * 6 + 2 * kind + (way - 1)
+            dst = slot_0.at[n, 2 * kind + way - 1]
+            now[kind, way] = copy(
+                acc.at[part(turn, flip, half, cols)],
+                view(dst, turn, wide), number, place.partner(turn, way),
+            )
+        landed.append(now)
+    for way, half in ((1, 0), (2, 1)):
+        for n, (_, cols, turn) in enumerate(pieces):
+            wide = slice(0, cols.stop - cols.start)
+            landed[n][0, way].wait_recv()
+            spot = part(turn, 3 - way, half, cols)
+            acc[spot] = acc[spot] + view(slot_0.at[n, way - 1], turn, wide)[...]
+            number = base + n * 6 + 4 + (2 - way)
+            landed[n][2, 3 - way] = copy(
+                acc.at[spot], view(slot_0.at[n, 4 + 2 - way], turn, wide), number,
+                place.partner(turn, 3 - way),
+            )
+    base += 6 * count
+    for n, (_, cols, turn) in enumerate(pieces):
+        wide = slice(0, cols.stop - cols.start)
+        for kind in (1, 2):
+            for way in (1, 2):
+                landed[n][kind, way].wait_recv()
+        for half in (0, 1):
+            spot = part(turn, 0, half, cols)
+            one, two = (2, 5) if half == 0 else (3, 4)
+            acc[spot] = acc[spot] + (
+                view(slot_0.at[n, one], turn, wide)[...] + view(slot_0.at[n, two], turn, wide)[...]
+            )
+    waiting = [[] for _ in pieces]
+    for n, (_, cols, turn) in enumerate(pieces):
+        wide = slice(0, cols.stop - cols.start)
+        group = (turn + 1) % 3
         for flip in (1, 2, 3):
-            src = acc.at[(*at_groups(turn, place.flipped(turn, flip)), every, cols)]
+            src = acc.at[(*at_groups(turn, place.q[turn], place.flipped(group, flip)), every, cols)]
             waiting[n].append(
-                copy(src, slot_0.at[n, flip - 1, :, :, :, 0 : cols.stop - cols.start],
-                     base + n * 3 + flip - 1, place.partner(turn, flip))
+                copy(src, slot_1.at[n, flip - 1, :, :, wide], base + n * 3 + flip - 1,
+                     place.partner(group, flip))
             )
     base += 3 * count
-    for phase in (1, 2):
-        for n, (rows, cols, turn) in enumerate(pieces):
-            wide = slice(0, cols.stop - cols.start)
-            q = [place.q[(turn + k) % 3] for k in range(3)]
-            for made in waiting[n]:
-                made.wait_recv()
-            started += waiting[n]
-            waiting[n] = []
-            group = (turn + phase) % 3
-            if phase == 1:
-                lead = at_groups(turn, q[0])
-                acc[(*lead, every, cols)] = (
-                    (acc[(*lead, every, cols)] + slot_0[n, 0, :, :, :, wide])
-                    + (slot_0[n, 1, :, :, :, wide] + slot_0[n, 2, :, :, :, wide])
-                )
-            else:
-                lead = at_groups(turn, q[0], q[1])
-                acc[(*lead, every, cols)] = (
-                    (acc[(*lead, every, cols)] + slot_1[n, 0, :, :, wide])
-                    + (slot_1[n, 1, :, :, wide] + slot_1[n, 2, :, :, wide])
-                )
-            for flip in (1, 2, 3):
-                theirs = place.flipped(group, flip)
-                if phase == 1:
-                    src = acc.at[(*at_groups(turn, q[0], theirs), every, cols)]
-                    dst = slot_1.at[n, flip - 1, :, :, wide]
-                else:
-                    src = acc.at[(*at_groups(turn, q[0], q[1], theirs), every, cols)]
-                    dst = slot_2.at[n, flip - 1, :, wide]
-                waiting[n].append(
-                    copy(src, dst, base + n * 3 + flip - 1, place.partner(group, flip))
-                )
-        base += 3 * count
-    for n, (rows, cols, turn) in enumerate(pieces):
+    for n, (_, cols, turn) in enumerate(pieces):
         wide = slice(0, cols.stop - cols.start)
         for made in waiting[n]:
             made.wait_recv()
-        started += waiting[n]
-        out_ref[(core, *place.q, every, cols)] = (
-            (acc[(*place.q, every, cols)] + slot_2[n, 0, :, wide])
-            + (slot_2[n, 1, :, wide] + slot_2[n, 2, :, wide])
+        waiting[n] = []
+        group = (turn + 2) % 3
+        spot = (*at_groups(turn, place.q[turn], place.q[(turn + 1) % 3]), every, cols)
+        acc[spot] = (acc[spot] + slot_1[n, 0, :, :, wide]) + (
+            slot_1[n, 1, :, :, wide] + slot_1[n, 2, :, :, wide]
         )
-    gather_phases(place, out_ref, pieces, (send_sem, recv_sem), base)
+        for flip in (1, 2, 3):
+            waiting[n].append(
+                copy(acc.at[spot], slot_2.at[n, flip - 1, :, :, wide], base + n * 3 + flip - 1,
+                     place.partner(group, flip))
+            )
+    base += 3 * count
+    for n, (_, cols, turn) in enumerate(pieces):
+        wide = slice(0, cols.stop - cols.start)
+        for made in waiting[n]:
+            made.wait_recv()
+        spot = (*at_groups(turn, place.q[turn], place.q[(turn + 1) % 3]), every, cols)
+        out_ref[(core, *spot)] = (acc[spot] + slot_2[n, 0, :, :, wide]) + (
+            slot_2[n, 1, :, :, wide] + slot_2[n, 2, :, :, wide]
+        )
+    gather_phases(place, out_ref, pieces, (send_sem, recv_sem), base, (1, 2))
     for made in started:
         made.wait_send()
+
+
+def view(ref, turn, wide):
+    shape = [None, None]
+    where = [(turn + 1) % 3, (turn + 2) % 3]
+    shape = (2, 4) if where[0] < where[1] else (4, 2)
+    return ref.reshape(*shape, *ref.shape[1:]).at[:, :, :, wide]
 
 
 def sum_grads(grads):
@@ -458,7 +513,7 @@
         (every, slice(share, 2 * share), 1),
         (every, slice(2 * share, width), 2),
     )
-    copies = (1 + 9 + 13) * len(pieces)
+    copies = (1 + 6 + 6 + GATHERS) * len(pieces)
     f32 = jnp.float32
     return pl.pallas_call(
         functools.partial(grads_kernel, pieces),
@@ -468,9 +523,9 @@
         scratch_shapes=[
             pltpu.VMEM(shape[1:], f32),
             pltpu.VMEM(shape[1:], f32),
-            pltpu.VMEM((3, 3, 4, 4, 8, share), f32),
+            pltpu.VMEM((3, 6, 8, 8, share), f32),
             pltpu.VMEM((3, 3, 4, 8, share), f32),
-            pltpu.VMEM((3, 3, 8, share), f32),
+            pltpu.VMEM((3, 3, 4, 8, share), f32),
             pltpu.SemaphoreType.DMA((copies,)),
             pltpu.SemaphoreType.DMA((copies,)),
         ],

time: 152 us -> 144 us (0.947)
  Pallas kernels: 140 us -> 132 us
    pallas_call x1, Pallas kernels: 51.6 us -> 46.9 us  [sum_grads(): pl.pallas_call(functools.partial(grads_kernel, pieces), out_shape=jax.Sha...]
    pallas_call x1, Pallas kernels: 67.4 us -> 64.4 us  [find_target(): pl.pallas_call(functools.partial(target_kernel, pieces, total_noise), out...]
where the time goes in v3:
time: 144 us
  Pallas kernels  132 us (92%)
  local copies, waits for them, and re-layouts  9.6 us (7%)
  other arithmetic  1.49 us (1%)
    pallas_call x1, Pallas kernels, find_target(): pl.pallas_call(functools.partial(target_kernel, pieces, total_noise), out...  64.4 us
    pallas_call x1, Pallas kernels, sum_grads(): pl.pallas_call(functools.partial(grads_kernel, pieces), out_shape=jax.Sha...  46.9 us
    pallas_call x1, Pallas kernels, train(): pl.pallas_call(functools.partial(train_kernel, scale, points, steps_each)...  20.7 us
    slice x2, local copies, waits for them, and re-layouts, on_device(): summed[1][:, k * width:(k + 1) * width]  4.17 us

profile of v3, /device:TPU:1, one launch (start us, length us, event | category | flops | bytes accessed | tf_op | source)
XLA Modules:
  0.0 143.8 jit_solution(3130297639091369300)
XLA Ops:
  0.6 0.8 copy.10
  1.5 0.1 broadcast_in_dim.7
  1.6 1.9 %constant_dynamic-slice_fusion.anchor_ref = f32[256,512]{1,0:T(8,128)} fusion(f32[4096,512]{1,0:T(8,128)} %noise_ref.1, s32[]{:T(128)S(6)} %select_n.3), kind=kLoop, calls=%fused_computation.1 | loop fusion | bytes 1048580 | tf_op jit(solution)/shard_map/dynamic_slice | solution.py:644
  3.5 0.0 copy-start
  3.5 64.4 %find_target.1.target_ref = f32[256,512]{1,0:T(8,128)} custom-call(f32[256,512]{1,0:T(8,128)} %data_ref.1, f32[4096,512]{1,0:T(8,128)} %noise_ref.1), custom_call_target="tpu_custom_call" | custom-call | tf_op jit(solution)/shard_map/find_target/pallas_call | solution.py:357
  67.8 1.3 broadcast_in_dim.8.tvals_ref
  69.2 0.0 copy-done
  69.2 1.3 copy.11
  70.5 20.7 %train.1 = (bf16[2048,512]{1,0:T(8,128)(2,1)}, f32[2,512,1024]{2,1,0:T(8,128)}) custom-call(f32[256,512]{1,0:T(8,128)} %constant_dynamic-slice_fusion.anchor_ref, f32[256,512]{1,0:T(8,128)} %find_target.1.target_ref, f32[2048,128]{1,0:T(8,128)} %broadcast_in_dim.8.tvals_ref, f32[1,1024]{1,0:T(1,128)} %bitcast.9, bf16[512,1024]{1,0:T(8,128)(2,1)} %w_in_ref.1, ...), custom_call_target="tpu_custom_call" | custom-call | tf_op jit(solution)/shard_map/train/pallas_call | solution.py:615
  91.2 46.9 %sum_grads.1 = f32[2,4,4,4,8,1024]{5,4,3,2,1,0:T(8,128)} custom-call(f32[2,4,4,4,8,1024]{5,4,3,2,1,0:T(8,128)} %bitcast.6), custom_call_target="tpu_custom_call" | custom-call | tf_op jit(solution)/shard_map/sum_grads/pallas_call | solution.py:518
  138.1 4.0 %fusion = (f32[1,4,4,4,8,1024]{5,4,3,2,1,0:T(8,128)S(1)}, f32[1,4,4,4,8,1024]{5,4,3,2,1,0:T(8,128)}) fusion(f32[2,4,4,4,8,1024]{5,4,3,2,1,0:T(8,128)} %sum_grads.1), kind=kLoop, calls=%fused_computation.2 | loop fusion | bytes 8388608 | tf_op jit(solution)/shard_map/slice | solution.py:655
  142.1 0.2 fusion.1
  142.3 1.5 %pad_maximum_fusion = f32[1024,512]{1,0:T(8,128)} fusion(f32[512,512]{1,0:T(8,128)S(1)} %get-tuple-element.10, f32[512,512]{1,0:T(8,128)S(1)} %get-tuple-element.9), kind=kLoop, calls=%fused_computation | loop fusion | flops 524288 | bytes 4194304 | tf_op jit(solution)/shard_map/concatenate | solution.py:654
Async XLA Ops:
  3.5 65.7 %copy-start = (bf16[1024,512]{1,0:T(8,128)(2,1)S(1)}, bf16[1024,512]{1,0:T(8,128)(2,1)}, u32[]{:S(2)}) copy-start(bf16[1024,512]{1,0:T(8,128)(2,1)} %w_out_ref.1) | copy-start | bytes 3145732

commit v4 on v3

--- a/solution.py
+++ b/solution.py
@@ -10,7 +10,7 @@
 
 ENTROPY = 0.05
 MESH = pl.DeviceIdType.MESH
-VMEM_CAP = 60 * 1024 * 1024
+VMEM_CAP = 54 * 1024 * 1024
 GATHERS = 19
 
 
@@ -51,17 +51,6 @@
         if flip % 2:
             lo = 1 - lo
         return hi * 2 + lo
-
-
-def meet(place):
-    barrier = pltpu.get_barrier_semaphore()
-    pl.semaphore_signal(barrier, inc=1, device_id=place.other_core(), device_id_type=MESH)
-    for group in range(3):
-        for flip in (1, 2, 3):
-            pl.semaphore_signal(
-                barrier, inc=1, device_id=place.partner(group, flip), device_id_type=MESH
-            )
-    pl.semaphore_wait(barrier, 10)
 
 
 def at_groups(turn, first=None, second=None, third=None):
@@ -143,7 +132,7 @@
         made.wait_send()
 
 
-def meet_all(place):
+def greet(place):
     barrier = pltpu.get_barrier_semaphore()
     known = [place.other_core()]
     for group, both in ((0, True), (1, False), (2, True)):
@@ -153,7 +142,7 @@
                 known.append(place.partner(group, flip, 1))
     for device in known:
         pl.semaphore_signal(barrier, inc=1, device_id=device, device_id_type=MESH)
-    pl.semaphore_wait(barrier, len(known))
+    return len(known)
 
 
 def joined(pairs):
@@ -215,32 +204,17 @@
     return own, other, started
 
 
-def target_kernel(
-    pieces, total_noise, data_ref, noise_ref, target_ref, data, data_hi, data_lo, anchor, anchor_hi,
-    anchor_lo, score, running, pairs, held, slots, local_sem, send_sem, recv_sem,
+def find_target(
+    place, pieces, total_noise, target_ref, data, data_hi, data_lo, anchor, anchor_hi, anchor_lo,
+    score, running, pairs, held, slots, send_sem, recv_sem,
 ):
-    place = Place()
     f32, bf16 = jnp.float32, jnp.bfloat16
-    rows = data.shape[4]
-    share, width = anchor.shape
+    width = anchor.shape[1]
     chunks, _, chunk = score.shape
     total_data = chunks * chunk
-    start = pl.multiple_of(place.row * rows, rows)
-    unit = data.at[(place.core, *place.q)]
-    bring = pltpu.make_async_copy(data_ref.at[pl.ds(start, rows)], unit, local_sem.at[0])
-    bring.start()
-    first = pl.multiple_of(place.col * share, share)
-    noise = pltpu.make_async_copy(noise_ref.at[pl.ds(first, share)], anchor, local_sem.at[1])
-    noise.start()
-    meet_all(place)
-    bring.wait()
-    noise.wait()
+    gather_phases(place, data, pieces, (send_sem, recv_sem), 0)
     x = anchor[...]
-    high = x.astype(bf16)
-    anchor_hi[...] = high
-    anchor_lo[...] = (x - high.astype(f32)).astype(bf16)
     noise_sq = jnp.sum(x * x, axis=1, keepdims=True)
-    gather_phases(place, data, pieces, (send_sem, recv_sem), 0)
 
     across = (((1,), (1,)), ((), ()))
     lanes = 128
@@ -333,61 +307,10 @@
     target_ref[...] = target_ref[...] / jnp.sum(running[...], axis=1, keepdims=True)
 
 
-def find_target(noise_points, data_points, total_noise, share):
-    count, width = data_points.shape
-    peers = lax.axis_size("row")
-    rows = count // peers
-    total_data = count * lax.axis_size("col")
-    quarter, tile = rows // 4, width // 4
-    every = slice(None)
-    last = slice(3 * quarter, rows)
-    pieces = (
-        (slice(0, quarter), every, 0),
-        (slice(quarter, 2 * quarter), every, 1),
-        (slice(2 * quarter, 3 * quarter), every, 2),
-        (last, slice(0, tile), 0),
-        (last, slice(tile, 2 * tile), 1),
-        (last, slice(2 * tile, width), 2),
-    )
-    copies = GATHERS * len(pieces) + 24
-    chunk = 8 * rows
-    chunks = total_data // chunk
-    f32, bf16 = jnp.float32, jnp.bfloat16
-    half = (2, total_data // 256, 128)
-    return pl.pallas_call(
-        functools.partial(target_kernel, pieces, total_noise),
-        out_shape=jax.ShapeDtypeStruct((share, width), f32),
-        in_specs=[pl.BlockSpec(memory_space=pl.ANY)] * 2,
-        out_specs=pl.BlockSpec(memory_space=pltpu.VMEM),
-        scratch_shapes=[
-            pltpu.VMEM((2, 4, 4, 4, rows, width), f32),
-            pltpu.VMEM((chunks, chunk, width), bf16),
-            pltpu.VMEM((chunks, chunk, width), bf16),
-            pltpu.VMEM((share, width), f32),
-            pltpu.VMEM((share, width), bf16),
-            pltpu.VMEM((share, width), bf16),
-            pltpu.VMEM((chunks, share, chunk), f32),
-            pltpu.VMEM((share, 128), f32),
-            pltpu.VMEM((2, *half), f32),
-            pltpu.VMEM((2, *half), f32),
-            pltpu.VMEM((3, 8, *half), f32),
-            pltpu.SemaphoreType.DMA((2,)),
-            pltpu.SemaphoreType.DMA((copies,)),
-            pltpu.SemaphoreType.DMA((copies,)),
-        ],
-        compiler_params=pltpu.CompilerParams(
-            collective_id=1, has_side_effects=True, vmem_limit_bytes=VMEM_CAP
-        ),
-        name="find_target",
-    )(data_points, noise_points)
-
-
-def grads_kernel(
-    pieces, in_ref, out_ref, acc, from_core, slot_0, slot_1, slot_2, send_sem, recv_sem
+def sum_grads(
+    place, pieces, in_ref, out_ref, acc, from_core, slot_0, slot_1, slot_2, send_sem, recv_sem
 ):
-    place = Place()
     core = place.core
-    meet(place)
     count = len(pieces)
 
     def copy(src, dst, number, device):
@@ -503,53 +426,19 @@
     return ref.reshape(*shape, *ref.shape[1:]).at[:, :, :, wide]
 
 
-def sum_grads(grads):
-    shape = grads.shape
-    width = shape[-1]
-    share = 128 * -(-width // 384)
-    every = slice(None)
-    pieces = (
-        (every, slice(0, share), 0),
-        (every, slice(share, 2 * share), 1),
-        (every, slice(2 * share, width), 2),
-    )
-    copies = (1 + 6 + 6 + GATHERS) * len(pieces)
-    f32 = jnp.float32
-    return pl.pallas_call(
-        functools.partial(grads_kernel, pieces),
-        out_shape=jax.ShapeDtypeStruct(shape, f32),
-        in_specs=[pl.BlockSpec(memory_space=pltpu.VMEM)],
-        out_specs=pl.BlockSpec(memory_space=pltpu.VMEM),
-        scratch_shapes=[
-            pltpu.VMEM(shape[1:], f32),
-            pltpu.VMEM(shape[1:], f32),
-            pltpu.VMEM((3, 6, 8, 8, share), f32),
-            pltpu.VMEM((3, 3, 4, 8, share), f32),
-            pltpu.VMEM((3, 3, 4, 8, share), f32),
-            pltpu.SemaphoreType.DMA((copies,)),
-            pltpu.SemaphoreType.DMA((copies,)),
-        ],
-        compiler_params=pltpu.CompilerParams(
-            collective_id=3, has_side_effects=True, vmem_limit_bytes=VMEM_CAP
-        ),
-        name="sum_grads",
-    )(grads)
-
-
 def spread(rows, steps_each):
     count, width = rows.shape
     wide = jnp.broadcast_to(rows[:, None, :], (count, steps_each, width))
     return wide.reshape(count * steps_each, width)
 
 
-def train_kernel(
+def train(
     scale, points, steps_each, anchor_ref, target_ref, tvals_ref, shift_ref, w_in_ref, w_out_ref,
     w_back_ref, predicted_ref, grads_ref, mixed_ref, hidden_ref, delta_ref, delta_pre_ref,
 ):
     block = points * steps_each
     width, hid_width = w_in_ref.shape
     blocks = anchor_ref.shape[0] // points
-    grads_ref[...] = jnp.zeros_like(grads_ref)
     f32, bf16 = jnp.float32, jnp.bfloat16
     contract = (((0,), (0,)), ((), ()))
     lanes = 128
@@ -603,58 +492,169 @@
     add_grads((blocks - 1) % 2)
 
 
-def train(anchor, target, times, time_shift, weight_in, weight_out, scale):
+def step_kernel(
+    data_pieces, grad_pieces, total_noise, points, data_ref, noise_ref, times_ref, shift_ref,
+    w_in_ref, w_out_ref, predicted_ref, grad_in_ref, grad_out_ref, data, data_hi, data_lo, anchor,
+    anchor_hi, anchor_lo, score, running, pairs, held, slots, target, w_in, w_out, w_back, steps,
+    tvals, mixed, hidden, delta, delta_pre, grads, acc, from_core, slot_0, slot_1,
+    slot_2, summed, local_sem, send_sem, recv_sem, grad_send_sem, grad_recv_sem,
+):
+    place = Place()
+    f32, bf16 = jnp.float32, jnp.bfloat16
+    rows = data.shape[4]
     share, width = anchor.shape
-    hid_width = weight_in.shape[1]
-    steps_each = times.shape[1]
+    hid_width = w_in.shape[1]
+    steps_each = times_ref.shape[0]
+    start = pl.multiple_of(place.row * rows, rows)
+    first = pl.multiple_of(place.col * share, share)
+    loads = [
+        pltpu.make_async_copy(source, to, local_sem.at[k])
+        for k, (source, to) in enumerate((
+            (data_ref.at[pl.ds(start, rows)], data.at[(place.core, *place.q)]),
+            (noise_ref.at[pl.ds(first, share)], anchor),
+            (w_out_ref, w_out),
+            (w_in_ref, w_in),
+        ))
+    ]
+    for load in loads:
+        load.start()
+    count = greet(place)
+    grads[...] = jnp.zeros_like(grads)
+    steps[...] = times_ref[...].T
+    block = points * steps_each
+
+    @pl.loop(0, share // points)
+    def _(b):
+        here = pl.ds(pl.multiple_of(b * points, points), points)
+        wide = spread(steps[here, :], steps_each)
+        row = lax.broadcasted_iota(jnp.int32, wide.shape, 0)
+        lane = lax.broadcasted_iota(jnp.int32, wide.shape, 1)
+        own = jnp.where(row % steps_each == lane, wide, 0.0)
+        value = jnp.sum(own, axis=1, keepdims=True)
+        to = pl.ds(pl.multiple_of(b * block, block), block)
+        tvals[to, :] = jnp.broadcast_to(value, (block, 128))
+
+    for load in loads:
+        load.wait()
+    x = anchor[...]
+    high = x.astype(bf16)
+    anchor_hi[...] = high
+    anchor_lo[...] = (x - high.astype(f32)).astype(bf16)
+    for k in range(hid_width // 256):
+        part = slice(k * 256, (k + 1) * 256)
+        w_back[:, part] = w_out[part, :].T
+    pl.semaphore_wait(pltpu.get_barrier_semaphore(), count)
+    find_target(
+        place, data_pieces, total_noise, target, data, data_hi, data_lo, anchor, anchor_hi,
+        anchor_lo, score, running, pairs, held, slots, send_sem, recv_sem,
+    )
+    scale = 1.0 / math.sqrt(float(total_noise * steps_each))
+    train(
+        scale, points, steps_each, anchor, target, tvals, shift_ref, w_in, w_out, w_back,
+        predicted_ref, grads, mixed, hidden, delta, delta_pre,
+    )
+    sum_grads(
+        place, grad_pieces, grads.reshape(summed.shape), summed, acc, from_core, slot_0, slot_1,
+        slot_2, grad_send_sem, grad_recv_sem,
+    )
+
+    @pl.loop(0, 16)
+    def _(i):
+        a, b = i // 4, i % 4
+        count = 4 * summed.shape[4]
+        to = pl.multiple_of(i * count, count)
+        grad_in_ref[pl.ds(to, count), :] = summed[0, a, b].reshape(count, hid_width)
+        for k in range(hid_width // width):
+            part = slice(k * width, (k + 1) * width)
+            here = pl.ds(pl.multiple_of(k * width + to, count), count)
+            grad_out_ref[here, :] = summed[1, a, b, :, :, part].reshape(count, width)
+
+
+def on_device(noise_points, data_points, times, time_shift, weight_in, weight_out):
+    count_row = lax.axis_size("row")
+    count_col = lax.axis_size("col")
+    total_noise = noise_points.shape[0] * count_row
+    total_data = data_points.shape[0] * count_col
+    width, hid_width = weight_in.shape
+    share, steps_each = times.shape
+    rows = data_points.shape[0] // count_row
+    chunk = 8 * rows
+    chunks = total_data // chunk
     points = 32
     block = points * steps_each
-    tvals = jnp.broadcast_to(times.reshape(share * steps_each, 1), (share * steps_each, 128))
-    bf16 = jnp.bfloat16
-    vmem = pl.BlockSpec(memory_space=pltpu.VMEM)
+    quarter, tile = rows // 4, width // 4
+    every = slice(None)
+    last = slice(3 * quarter, rows)
+    data_pieces = (
+        (slice(0, quarter), every, 0),
+        (slice(quarter, 2 * quarter), every, 1),
+        (slice(2 * quarter, 3 * quarter), every, 2),
+        (last, slice(0, tile), 0),
+        (last, slice(tile, 2 * tile), 1),
+        (last, slice(2 * tile, width), 2),
+    )
+    third = 128 * -(-hid_width // 384)
+    grad_pieces = (
+        (every, slice(0, third), 0),
+        (every, slice(third, 2 * third), 1),
+        (every, slice(2 * third, hid_width), 2),
+    )
+    copies = GATHERS * len(data_pieces) + 24
+    grad_copies = (1 + 6 + 6 + GATHERS) * len(grad_pieces)
+    f32, bf16 = jnp.float32, jnp.bfloat16
+    pair = (2, total_data // 256, 128)
+    units = (4, 4, 4, width // 64, hid_width)
+    far = pl.BlockSpec(memory_space=pl.ANY)
+    near = pl.BlockSpec(memory_space=pltpu.VMEM)
     return pl.pallas_call(
-        functools.partial(train_kernel, scale, points, steps_each),
+        functools.partial(step_kernel, data_pieces, grad_pieces, total_noise, points),
         out_shape=(
-            jax.ShapeDtypeStruct((share * steps_each, width), bf16),
-            jax.ShapeDtypeStruct((2, width, hid_width), jnp.float32),
+            pltpu.VMEM((share * steps_each, width), bf16),
+            pltpu.VMEM((width, hid_width), f32),
+            pltpu.VMEM((hid_width, width), f32),
         ),
-        in_specs=[vmem] * 7,
-        out_specs=(vmem, vmem),
+        in_specs=[far, far, near, near, far, far],
+        out_specs=(near, near, near),
         scratch_shapes=[
+            pltpu.VMEM((2, 4, 4, 4, rows, width), f32),
+            pltpu.VMEM((chunks, chunk, width), bf16),
+            pltpu.VMEM((chunks, chunk, width), bf16),
+            pltpu.VMEM((share, width), f32),
+            pltpu.VMEM((share, width), bf16),
+            pltpu.VMEM((share, width), bf16),
+            pltpu.VMEM((chunks, share, chunk), f32),
+            pltpu.VMEM((share, 128), f32),
+            pltpu.VMEM((2, *pair), f32),
+            pltpu.VMEM((2, *pair), f32),
+            pltpu.VMEM((3, 8, *pair), f32),
+            pltpu.VMEM((share, width), f32),
+            pltpu.VMEM((width, hid_width), bf16),
+            pltpu.VMEM((hid_width, width), bf16),
+            pltpu.VMEM((width, hid_width), bf16),
+            pltpu.VMEM((share, steps_each), f32),
+            pltpu.VMEM((share * steps_each, 128), f32),
             pltpu.VMEM((2, block, width), bf16),
             pltpu.VMEM((2, block, hid_width), bf16),
             pltpu.VMEM((2, block, width), bf16),
             pltpu.VMEM((2, block, hid_width), bf16),
+            pltpu.VMEM((2, width, hid_width), f32),
+            pltpu.VMEM(units, f32),
+            pltpu.VMEM(units, f32),
+            pltpu.VMEM((3, 6, 8, width // 64, third), f32),
+            pltpu.VMEM((3, 3, 4, width // 64, third), f32),
+            pltpu.VMEM((3, 3, 4, width // 64, third), f32),
+            pltpu.VMEM((2, *units), f32),
+            pltpu.SemaphoreType.DMA((4,)),
+            pltpu.SemaphoreType.DMA((copies,)),
+            pltpu.SemaphoreType.DMA((copies,)),
+            pltpu.SemaphoreType.DMA((grad_copies,)),
+            pltpu.SemaphoreType.DMA((grad_copies,)),
         ],
-        compiler_params=pltpu.CompilerParams(vmem_limit_bytes=VMEM_CAP),
-        name="train",
-    )(anchor, target, tvals, time_shift.reshape(1, hid_width), weight_in, weight_out, weight_out.T)
-
-
-def on_device(noise_points, data_points, times, time_shift, weight_in, weight_out):
-    count_row = lax.axis_size("row")
-    count_col = lax.axis_size("col")
-    rows_here = noise_points.shape[0]
-    total_noise = rows_here * count_row
-    width = noise_points.shape[1]
-    share = rows_here // count_col
-    steps_each = times.shape[1]
-
-    target = find_target(noise_points, data_points, total_noise, share)
-    anchor = lax.dynamic_slice_in_dim(noise_points, lax.axis_index("col") * share, share, 0)
-    scale = 1.0 / math.sqrt(float(total_noise * steps_each))
-    predicted, grads = train(
-        anchor, target, times, time_shift, weight_in, weight_out, scale
-    )
-    hid_width = weight_in.shape[1]
-    halves = hid_width // width
-    grads = grads.reshape(2, 4, 4, 4, width // 64, hid_width)
-    summed = sum_grads(grads).reshape(2, width, hid_width)
-    grad_in = summed[0]
-    grad_out = jnp.concatenate(
-        [summed[1][:, k * width : (k + 1) * width] for k in range(halves)], axis=0
-    )
-    return (predicted, grad_in, grad_out)
+        compiler_params=pltpu.CompilerParams(
+            collective_id=1, has_side_effects=True, vmem_limit_bytes=VMEM_CAP
+        ),
+        name="step",
+    )(data_points, noise_points, times.T, time_shift.reshape(1, hid_width), weight_in, weight_out)
 
 
 def solution(mesh):

time: 144 us -> 126 us (0.88)
  Pallas kernels: 132 us -> 122 us
  local copies, waits for them, and re-layouts: 9.6 us -> 3.96 us
  other arithmetic: 1.49 us -> 0 us
    pallas_call x3 -> x1, Pallas kernels: 132 us -> 122 us  [on_device(): pl.pallas_call(functools.partial(step_kernel, data_pieces, grad_pieces, t...]
    slice x2 -> x0, local copies, waits for them, and re-layouts: 4.17 us -> none  [on_device(): summed[1][:, k * width:(k + 1) * width]]
    dynamic_slice x1 -> x0, local copies, waits for them, and re-layouts: 1.89 us -> none  [on_device(): lax.dynamic_slice_in_dim(noise_points, lax.axis_index('col') * share, sha...]
    unnamed x4 -> x3, local copies, waits for them, and re-layouts: 2.13 us -> 3.96 us
    concatenate x1 -> x0, other arithmetic: 1.49 us -> none  [on_device(): jnp.concatenate([summed[1][:, k * width:(k + 1) * width] for k in range(h...]
where the time goes in v4:
time: 126 us
  Pallas kernels  122 us (97%)
  local copies, waits for them, and re-layouts  3.96 us (3%)
    pallas_call x1, Pallas kernels, on_device(): pl.pallas_call(functools.partial(step_kernel, data_pieces, grad_pieces, t...  122 us
    unnamed x3, local copies, waits for them, and re-layouts  3.96 us

profile of v4, /device:TPU:1, one launch (start us, length us, event | category | flops | bytes accessed | tf_op | source)
XLA Modules:
  0.0 126.2 jit_solution(12638324719557445710)
XLA Ops:
  0.6 121.6 %step.1 = (bf16[2048,512]{1,0:T(8,128)(2,1)S(1)}, f32[512,1024]{1,0:T(8,128)S(1)}, f32[1024,512]{1,0:T(8,128)S(1)}) custom-call(f32[256,512]{1,0:T(8,128)} %data_ref.1, f32[4096,512]{1,0:T(8,128)} %noise_ref.1, f32[8,256]{1,0:T(8,128)} %bitcast.2, f32[1,1024]{1,0:T(1,128)} %bitcast.3, bf16[512,1024]{1,0:T(8,128)(2,1)} %w_in_ref.1, bf16[1024,512]{1,0:T(8,128)(2,1)} %w_out_ref.1), custom_call_target="tpu_custom_call" | custom-call | tf_op jit(solution)/shard_map/step/pallas_call | solution.py:609
  122.2 1.3 %copy.12 = bf16[2048,512]{1,0:T(8,128)(2,1)} copy(bf16[2048,512]{1,0:T(8,128)(2,1)S(1)} %get-tuple-element.3) | data formatting | bytes 4194304
  123.5 1.3 %copy.13 = f32[512,1024]{1,0:T(8,128)} copy(f32[512,1024]{1,0:T(8,128)S(1)} %get-tuple-element.4) | data formatting | bytes 4194304
  124.8 1.3 %copy.14 = f32[1024,512]{1,0:T(8,128)} copy(f32[1024,512]{1,0:T(8,128)S(1)} %get-tuple-element.5) | data formatting | bytes 4194304

commit v5 on v4

--- a/solution.py
+++ b/solution.py
@@ -61,7 +61,7 @@
     return tuple(found)
 
 
-def gather_phases(place, out, pieces, sems, base, phases=(0, 1, 2)):
+def gather_phases(place, out, pieces, sems, base, phases=(0, 1, 2), meanwhile=None):
     send, recv = sems
     mine = out.at[place.core]
     started = []
@@ -92,6 +92,8 @@
             for flip in (1, 2, 3):
                 number = base + GATHERS * n + phase * 3 + flip - 1
                 waiting[n].append(copy(block, number, place.partner(group, flip)))
+        if phase == phases[0] and meanwhile is not None:
+            meanwhile()
     halves = (pl.ds(0, 2), pl.ds(2, 2))
     across, landed = [], []
     for n, piece in enumerate(pieces):
@@ -206,13 +208,13 @@
 
 def find_target(
     place, pieces, total_noise, target_ref, data, data_hi, data_lo, anchor, anchor_hi, anchor_lo,
-    score, running, pairs, held, slots, send_sem, recv_sem,
+    score, running, pairs, held, slots, send_sem, recv_sem, meanwhile,
 ):
     f32, bf16 = jnp.float32, jnp.bfloat16
     width = anchor.shape[1]
     chunks, _, chunk = score.shape
     total_data = chunks * chunk
-    gather_phases(place, data, pieces, (send_sem, recv_sem), 0)
+    gather_phases(place, data, pieces, (send_sem, recv_sem), 0, meanwhile=meanwhile)
     x = anchor[...]
     noise_sq = jnp.sum(x * x, axis=1, keepdims=True)
 
@@ -484,20 +486,24 @@
 
     forward(0, 0)
 
-    @pl.loop(1, blocks)
-    def _(b):
-        forward(b, b % 2)
-        add_grads((b + 1) % 2)
-
-    add_grads((blocks - 1) % 2)
+    @pl.loop(0, blocks // 2 - 1)
+    def _(j):
+        forward(2 * j + 1, 1)
+        add_grads(0)
+        forward(2 * j + 2, 0)
+        add_grads(1)
+
+    forward(blocks - 1, 1)
+    add_grads(0)
+    add_grads(1)
 
 
 def step_kernel(
     data_pieces, grad_pieces, total_noise, points, data_ref, noise_ref, times_ref, shift_ref,
-    w_in_ref, w_out_ref, predicted_ref, grad_in_ref, grad_out_ref, data, data_hi, data_lo, anchor,
+    w_in_ref, w_out_ref, predicted_ref, summed, data, data_hi, data_lo, anchor,
     anchor_hi, anchor_lo, score, running, pairs, held, slots, target, w_in, w_out, w_back, steps,
     tvals, mixed, hidden, delta, delta_pre, grads, acc, from_core, slot_0, slot_1,
-    slot_2, summed, local_sem, send_sem, recv_sem, grad_send_sem, grad_recv_sem,
+    slot_2, local_sem, send_sem, recv_sem, grad_send_sem, grad_recv_sem,
 ):
     place = Place()
     f32, bf16 = jnp.float32, jnp.bfloat16
@@ -519,34 +525,38 @@
     for load in loads:
         load.start()
     count = greet(place)
-    grads[...] = jnp.zeros_like(grads)
-    steps[...] = times_ref[...].T
     block = points * steps_each
 
-    @pl.loop(0, share // points)
-    def _(b):
-        here = pl.ds(pl.multiple_of(b * points, points), points)
-        wide = spread(steps[here, :], steps_each)
-        row = lax.broadcasted_iota(jnp.int32, wide.shape, 0)
-        lane = lax.broadcasted_iota(jnp.int32, wide.shape, 1)
-        own = jnp.where(row % steps_each == lane, wide, 0.0)
-        value = jnp.sum(own, axis=1, keepdims=True)
-        to = pl.ds(pl.multiple_of(b * block, block), block)
-        tvals[to, :] = jnp.broadcast_to(value, (block, 128))
-
-    for load in loads:
-        load.wait()
-    x = anchor[...]
-    high = x.astype(bf16)
-    anchor_hi[...] = high
-    anchor_lo[...] = (x - high.astype(f32)).astype(bf16)
-    for k in range(hid_width // 256):
-        part = slice(k * 256, (k + 1) * 256)
-        w_back[:, part] = w_out[part, :].T
+    def prepare():
+        grads[...] = jnp.zeros_like(grads)
+        steps[...] = times_ref[...].T
+
+        @pl.loop(0, share // points)
+        def _(b):
+            here = pl.ds(pl.multiple_of(b * points, points), points)
+            wide = spread(steps[here, :], steps_each)
+            row = lax.broadcasted_iota(jnp.int32, wide.shape, 0)
+            lane = lax.broadcasted_iota(jnp.int32, wide.shape, 1)
+            own = jnp.where(row % steps_each == lane, wide, 0.0)
+            value = jnp.sum(own, axis=1, keepdims=True)
+            to = pl.ds(pl.multiple_of(b * block, block), block)
+            tvals[to, :] = jnp.broadcast_to(value, (block, 128))
+
+        for load in loads[1:]:
+            load.wait()
+        x = anchor[...]
+        high = x.astype(bf16)
+        anchor_hi[...] = high
+        anchor_lo[...] = (x - high.astype(f32)).astype(bf16)
+        for k in range(hid_width // 256):
+            part = slice(k * 256, (k + 1) * 256)
+            w_back[:, part] = w_out[part, :].T
+
+    loads[0].wait()
     pl.semaphore_wait(pltpu.get_barrier_semaphore(), count)
     find_target(
         place, data_pieces, total_noise, target, data, data_hi, data_lo, anchor, anchor_hi,
-        anchor_lo, score, running, pairs, held, slots, send_sem, recv_sem,
+        anchor_lo, score, running, pairs, held, slots, send_sem, recv_sem, prepare,
     )
     scale = 1.0 / math.sqrt(float(total_noise * steps_each))
     train(
@@ -558,16 +568,19 @@
         slot_2, grad_send_sem, grad_recv_sem,
     )
 
-    @pl.loop(0, 16)
-    def _(i):
-        a, b = i // 4, i % 4
-        count = 4 * summed.shape[4]
-        to = pl.multiple_of(i * count, count)
-        grad_in_ref[pl.ds(to, count), :] = summed[0, a, b].reshape(count, hid_width)
-        for k in range(hid_width // width):
-            part = slice(k * width, (k + 1) * width)
-            here = pl.ds(pl.multiple_of(k * width + to, count), count)
-            grad_out_ref[here, :] = summed[1, a, b, :, :, part].reshape(count, width)
+
+def store_kernel(predicted, summed, predicted_ref, grad_in_ref, grad_out_ref, sem):
+    width, hid_width = grad_in_ref.shape
+    result = summed.reshape(2, width, hid_width)
+    moves = [(predicted, predicted_ref), (result.at[0], grad_in_ref)]
+    for k in range(hid_width // width):
+        part = slice(k * width, (k + 1) * width)
+        moves.append((result.at[1, :, part], grad_out_ref.at[part]))
+    made = [pltpu.make_async_copy(a, b, sem.at[k]) for k, (a, b) in enumerate(moves)]
+    for copy in made:
+        copy.start()
+    for copy in made:
+        copy.wait()
 
 
 def on_device(noise_points, data_points, times, time_shift, weight_in, weight_out):
@@ -599,6 +612,7 @@
         (every, slice(third, 2 * third), 1),
         (every, slice(2 * third, hid_width), 2),
     )
+    parts = len(grad_pieces)
     copies = GATHERS * len(data_pieces) + 24
     grad_copies = (1 + 6 + 6 + GATHERS) * len(grad_pieces)
     f32, bf16 = jnp.float32, jnp.bfloat16
@@ -606,15 +620,14 @@
     units = (4, 4, 4, width // 64, hid_width)
     far = pl.BlockSpec(memory_space=pl.ANY)
     near = pl.BlockSpec(memory_space=pltpu.VMEM)
-    return pl.pallas_call(
+    predicted, summed = pl.pallas_call(
         functools.partial(step_kernel, data_pieces, grad_pieces, total_noise, points),
         out_shape=(
             pltpu.VMEM((share * steps_each, width), bf16),
-            pltpu.VMEM((width, hid_width), f32),
-            pltpu.VMEM((hid_width, width), f32),
+            pltpu.VMEM((2, *units), f32),
         ),
         in_specs=[far, far, near, near, far, far],
-        out_specs=(near, near, near),
+        out_specs=(near, near),
         scratch_shapes=[
             pltpu.VMEM((2, 4, 4, 4, rows, width), f32),
             pltpu.VMEM((chunks, chunk, width), bf16),
@@ -640,10 +653,9 @@
             pltpu.VMEM((2, width, hid_width), f32),
             pltpu.VMEM(units, f32),
             pltpu.VMEM(units, f32),
-            pltpu.VMEM((3, 6, 8, width // 64, third), f32),
-            pltpu.VMEM((3, 3, 4, width // 64, third), f32),
-            pltpu.VMEM((3, 3, 4, width // 64, third), f32),
-            pltpu.VMEM((2, *units), f32),
+            pltpu.VMEM((parts, 6, 8, width // 64, third), f32),
+            pltpu.VMEM((parts, 3, 4, width // 64, third), f32),
+            pltpu.VMEM((parts, 3, 4, width // 64, third), f32),
             pltpu.SemaphoreType.DMA((4,)),
             pltpu.SemaphoreType.DMA((copies,)),
             pltpu.SemaphoreType.DMA((copies,)),
@@ -655,6 +667,19 @@
         ),
         name="step",
     )(data_points, noise_points, times.T, time_shift.reshape(1, hid_width), weight_in, weight_out)
+    return pl.pallas_call(
+        store_kernel,
+        out_shape=(
+            jax.ShapeDtypeStruct((share * steps_each, width), bf16),
+            jax.ShapeDtypeStruct((width, hid_width), f32),
+            jax.ShapeDtypeStruct((hid_width, width), f32),
+        ),
+        in_specs=[near, near],
+        out_specs=(far, far, far),
+        scratch_shapes=[pltpu.SemaphoreType.DMA((2 + hid_width // width,))],
+        compiler_params=pltpu.CompilerParams(vmem_limit_bytes=1024 * 1024),
+        name="store",
+    )(*(pltpu.with_memory_space_constraint(a, pltpu.VMEM) for a in (predicted, summed)))
 
 
 def solution(mesh):

time: 126 us -> 122 us (0.968)
  local copies, waits for them, and re-layouts: 3.96 us -> 0 us
    unnamed x3 -> x0, local copies, waits for them, and re-layouts: 3.96 us -> none
    pallas_call x1, Pallas kernels: 122 us -> 119 us  [on_device(): pl.pallas_call(functools.partial(step_kernel, data_pieces, grad_pieces, t...]
    pallas_call x0 -> x1, Pallas kernels: none -> 2.7 us  [on_device(): pl.pallas_call(store_kernel, out_shape=(jax.ShapeDtypeStruct((share * ste...]
where the time goes in v5:
time: 122 us
  Pallas kernels  121 us (99%)
    pallas_call x1, Pallas kernels, on_device(): pl.pallas_call(functools.partial(step_kernel, data_pieces, grad_pieces, t...  119 us
    pallas_call x1, Pallas kernels, on_device(): pl.pallas_call(store_kernel, out_shape=(jax.ShapeDtypeStruct((share * ste...  2.7 us

profile of v5, /device:TPU:1, one launch (start us, length us, event | category | flops | bytes accessed | tf_op | source)
XLA Modules:
  0.0 122.0 jit_solution(18364225125230568939)
XLA Ops:
  0.6 118.7 %step.1 = (bf16[2048,512]{1,0:T(8,128)(2,1)S(1)}, f32[2,4,4,4,8,1024]{5,4,3,2,1,0:T(8,128)S(1)}) custom-call(f32[256,512]{1,0:T(8,128)} %data_ref.1, f32[4096,512]{1,0:T(8,128)} %noise_ref.1, f32[8,256]{1,0:T(8,128)} %bitcast.2, f32[1,1024]{1,0:T(1,128)} %bitcast.3, bf16[512,1024]{1,0:T(8,128)(2,1)} %w_in_ref.1, bf16[1024,512]{1,0:T(8,128)(2,1)} %w_out_ref.1), custom_call_target="tpu_custom_call" | custom-call | tf_op jit(solution)/shard_map/step/pallas_call | solution.py:623
  119.3 2.7 %store.1 = (bf16[2048,512]{1,0:T(8,128)(2,1)}, f32[512,1024]{1,0:T(8,128)}, f32[1024,512]{1,0:T(8,128)}) custom-call(bf16[2048,512]{1,0:T(8,128)(2,1)S(1)} %get-tuple-element.5.predicted, f32[2,4,4,4,8,1024]{5,4,3,2,1,0:T(8,128)S(1)} %get-tuple-element.6.summed), custom_call_target="tpu_custom_call" | custom-call | tf_op jit(solution)/shard_map/store/pallas_call | solution.py:670

commit v6 on v5

--- a/solution.py
+++ b/solution.py
@@ -223,7 +223,7 @@
     tiles = chunk // lanes
     running[...] = jnp.full_like(running, -jnp.inf)
 
-    @pl.loop(0, chunks)
+    @pl.loop(0, chunks, unroll=2)
     def _(i):
         points = data[i // 8, (i // 2) % 4, pl.ds((i % 2) * 2, 2)].reshape(chunk, width)
         high = points.astype(bf16)
@@ -249,7 +249,7 @@
     peak = jnp.max(running[...], axis=1, keepdims=True)
     running[...] = jnp.zeros_like(running)
 
-    @pl.loop(0, chunks)
+    @pl.loop(0, chunks, unroll=2)
     def _(i):
         e = jnp.exp(score[i] - peak)
         total = running[...]
@@ -260,7 +260,7 @@
     total = jnp.sum(running[...], axis=1, keepdims=True)
     row_lse = peak + jnp.log(total) - math.log(float(total_data))
 
-    @pl.loop(0, chunks)
+    @pl.loop(0, chunks, unroll=2)
     def _(i):
         s = score[i] - row_lse
         col_peak = jnp.max(s, axis=0, keepdims=True)
@@ -280,7 +280,7 @@
     pairs[1 - place.core, 0] = other[0] + jnp.log(other[1]) - log_noise
     running[...] = jnp.full_like(running, -jnp.inf)
 
-    @pl.loop(0, chunks)
+    @pl.loop(0, chunks, unroll=2)
     def _(i):
         peak = running[...]
         for k in range(tiles):
@@ -295,7 +295,7 @@
     running[...] = jnp.zeros_like(running)
     target_ref[...] = jnp.zeros_like(target_ref)
 
-    @pl.loop(0, chunks)
+    @pl.loop(0, chunks, unroll=2)
     def _(i):
         weights = jnp.exp(score[i] - peak).astype(bf16)
         total = running[...]

time: 122 us -> 119 us (0.975)
  Pallas kernels: 121 us -> 118 us
    pallas_call x1, Pallas kernels: 119 us -> 115 us  [on_device(): pl.pallas_call(functools.partial(step_kernel, data_pieces, grad_pieces, t...]
where the time goes in v6:
time: 119 us
  Pallas kernels  118 us (99%)
    pallas_call x1, Pallas kernels, on_device(): pl.pallas_call(functools.partial(step_kernel, data_pieces, grad_pieces, t...  115 us
    pallas_call x1, Pallas kernels, on_device(): pl.pallas_call(store_kernel, out_shape=(jax.ShapeDtypeStruct((share * ste...  2.7 us

profile of v6, /device:TPU:1, one launch (start us, length us, event | category | flops | bytes accessed | tf_op | source)
XLA Modules:
  0.0 118.6 jit_solution(652946983672488662)
XLA Ops:
  0.6 115.2 %step.1 = (bf16[2048,512]{1,0:T(8,128)(2,1)S(1)}, f32[2,4,4,4,8,1024]{5,4,3,2,1,0:T(8,128)S(1)}) custom-call(f32[256,512]{1,0:T(8,128)} %data_ref.1, f32[4096,512]{1,0:T(8,128)} %noise_ref.1, f32[8,256]{1,0:T(8,128)} %bitcast.2, f32[1,1024]{1,0:T(1,128)} %bitcast.3, bf16[512,1024]{1,0:T(8,128)(2,1)} %w_in_ref.1, bf16[1024,512]{1,0:T(8,128)(2,1)} %w_out_ref.1), custom_call_target="tpu_custom_call" | custom-call | tf_op jit(solution)/shard_map/step/pallas_call | solution.py:623
  115.9 2.7 %store.1 = (bf16[2048,512]{1,0:T(8,128)(2,1)}, f32[512,1024]{1,0:T(8,128)}, f32[1024,512]{1,0:T(8,128)}) custom-call(bf16[2048,512]{1,0:T(8,128)(2,1)S(1)} %get-tuple-element.5.predicted, f32[2,4,4,4,8,1024]{5,4,3,2,1,0:T(8,128)S(1)} %get-tuple-element.6.summed), custom_call_target="tpu_custom_call" | custom-call | tf_op jit(solution)/shard_map/store/pallas_call | solution.py:670
